TPU v7x, 8 devices: a whole 2x2x1 slice. The times are simulated.
8 devices in a mesh: dp: 2 (over z, y), sp: 4 (over x, core).
Axes of the slice: x: 2, y: 2, z: 1, core: 2. Of those that a mesh axis runs over, the one named last changes fastest.
Arguments:
- images: bfloat16 [64, 32, 256, 32], P('dp', 'sp'), parts along dimension 0
- w_a: bfloat16 [2, 3, 3, 32, 32], replicated
- bn_a: float32 [2, 2, 32], replicated
- w_down: bfloat16 [3, 3, 32, 128], replicated
- bn_down: float32 [2, 128], replicated
- w_in: bfloat16 [3, 128, 64], replicated
- bn_in: float32 [3, 2, 64], replicated
- w_mid: bfloat16 [3, 3, 3, 64, 64], replicated
- bn_mid: float32 [3, 2, 64], replicated
- w_out: bfloat16 [3, 64, 128], replicated
- bn_out: float32 [3, 2, 128], replicated
Outputs:
- output: bfloat16 [64, 16, 128, 128], P('dp', 'sp'), parts along dimension 0
There are 2 independent parts. A program takes and returns all parts, laid end to end along the dimension named above; an argument that names none is the same for every part.
All inputs are finite; a program needn't handle non-finite values.
Results may differ from a plain program's by a relative error of at most 0.0191559.
Values are sent between devices in bfloat16 or wider.
A program may use at most 1 GiB of HBM per device.

v0:
```python
import jax
import jax.numpy as jnp
from jax import lax
from jax.sharding import PartitionSpec as P, NamedSharding

NORM_EPS = 1e-5
CONV_DIMS = ("NHWC", "HWIO", "NHWC")


def solution(mesh):
    groups = mesh.shape["sp"]
    to_next = [(device, device + 1) for device in range(groups - 1)]
    to_prev = [(device + 1, device) for device in range(groups - 1)]

    def conv_same(hidden, weight):
        from_above = lax.ppermute(hidden[:, -1:], "sp", to_next)
        from_below = lax.ppermute(hidden[:, :1], "sp", to_prev)
        padded = jnp.concatenate([from_above, hidden, from_below], axis=1)
        return lax.conv_general_dilated(padded, weight, (1, 1), ((0, 0), (1, 1)), dimension_numbers=CONV_DIMS, preferred_element_type=jnp.float32)

    def conv_down(hidden, weight):
        from_below = lax.ppermute(hidden[:, :1], "sp", to_prev)
        padded = jnp.concatenate([hidden, from_below], axis=1)
        return lax.conv_general_dilated(padded, weight, (2, 2), ((0, 0), (0, 1)), dimension_numbers=CONV_DIMS, preferred_element_type=jnp.float32)

    def conv_point(hidden, weight):
        return jnp.einsum("bhwc,cd->bhwd", hidden, weight, preferred_element_type=jnp.float32)

    def batch_norm(pre_act, params):
        norm_count = pre_act.shape[0] * pre_act.shape[1] * pre_act.shape[2] * groups
        part_sums = jnp.stack([jnp.sum(pre_act, axis=(0, 1, 2)), jnp.sum(pre_act * pre_act, axis=(0, 1, 2))])
        group_moments = lax.psum(part_sums, "sp") / norm_count
        chan_mean = group_moments[0]
        chan_var = group_moments[1] - chan_mean * chan_mean
        chan_scale = params[0] * lax.rsqrt(chan_var + NORM_EPS)
        return (pre_act - chan_mean) * chan_scale + params[1]

    def norm_relu(pre_act, params):
        return jax.nn.relu(batch_norm(pre_act, params)).astype(jnp.bfloat16)

    def forward(images, w_a, bn_a, w_down, bn_down, w_in, bn_in, w_mid, bn_mid, w_out, bn_out):
        hidden = images
        for layer_num in range(w_a.shape[0]):
            hidden = norm_relu(conv_same(hidden, w_a[layer_num]), bn_a[layer_num])
        hidden = norm_relu(conv_down(hidden, w_down), bn_down)
        for block_num in range(w_in.shape[0]):
            branch = norm_relu(conv_point(hidden, w_in[block_num]), bn_in[block_num])
            branch = norm_relu(conv_same(branch, w_mid[block_num]), bn_mid[block_num])
            summed = batch_norm(conv_point(branch, w_out[block_num]), bn_out[block_num]) + hidden
            hidden = jax.nn.relu(summed).astype(jnp.bfloat16)
        return hidden

    act_spec = P("dp", "sp", None, None)
    return jax.shard_map(forward, mesh=mesh, in_specs=(act_spec,) + (P(),) * 10, out_specs=act_spec, check_vma=False)
```

profile of v0, /device:TPU:0, one launch (start us, length us, event | category | flops | bytes accessed | tf_op | source)
XLA Modules:
  0.0 499.9 jit_solution(1631649009061777652)
XLA Ops:
  1.3 2.8 collective-permute-start
  6.1 3.9 collective-permute-done.1
  10.0 5.2 %pad_maximum_fusion = bf16[32,10,256,32]{2,3,1,0:T(8,128)(2,1)} fusion(bf16[32,1,256,32]{2,3,1,0:T(8,128)(2,1)S(1)} %collective-permute-done.1, bf16[32,8,256,32]{2,3,1,0:T(8,128)(2,1)} %param.11, bf16[32,1,256,32]{2,3,1,0:T(8,128)(2,1)S(1)} %collective-permute-done), kind=kLoop, calls=%fused_computation.40 | loop fusion | flops 5242880 | bytes 10485760 | tf_op jit(solution)/shard_map/concatenate | solution.py:18
  15.1 28.5 %copy.49 = bf16[32,10,256,32]{3,0,2,1:T(8,128)(2,1)} copy(bf16[32,10,256,32]{2,3,1,0:T(8,128)(2,1)} %pad_maximum_fusion) | data formatting | bytes 10485760 | tf_op jit(solution)/shard_map/concatenate | solution.py:18
  43.7 30.0 %fusion.114 = (f32[32]{0:T(128)S(1)}, f32[32]{0:T(128)S(1)}, f32[32,8,256,32]{3,0,2,1:T(8,128)}) fusion(bf16[32,10,256,32]{3,0,2,1:T(8,128)(2,1)} %copy.49, bf16[2,3,3,32,32]{4,3,2,1,0:T(8,128)(2,1)S(1)} %copy-done.13), kind=kOutput, calls=%fused_computation.202 | convolution fusion | flops 1211105280 | bytes 13705472 | tf_op jit(solution)/shard_map/conv_general_dilated | solution.py:19
  73.6 13.0 %psum.84 = f32[2,32]{1,0:T(2,128)S(1)} all-reduce(f32[2,32]{1,0:T(2,128)S(1)} %pad_maximum_fusion.4), channel_id=1, replica_groups=mesh['dp'=2,'sp'=4] {'sp'}, use_global_device_ids=true, to_apply=%region_2.0 | all-reduce | flops 64 | bytes 512 | tf_op jit(solution)/shard_map/psum | solution.py:32
  86.7 13.7 %maximum_convert_fusion.1 = bf16[32,8,256,32]{3,0,2,1:T(8,128)(2,1)S(1)} fusion(f32[32,8,256,32]{3,0,2,1:T(8,128)} %get-tuple-element.50, f32[32]{0:T(128)S(1)} %get-tuple-element.49, f32[32]{0:T(128)S(1)} %fusion.107, f32[32]{0:T(128)S(1)} %slice_bitcast_fusion.23), kind=kLoop, calls=%fused_computation.2 | loop fusion | flops 10485760 | bytes 12583296 | tf_op jit(solution)/shard_map/convert_element_type | solution.py:39
  100.4 5.7 %copy-done.4 = bf16[32,8,256,32]{3,0,2,1:T(8,128)(2,1)} copy-done((bf16[32,8,256,32]{3,0,2,1:T(8,128)(2,1)}, bf16[32,8,256,32]{3,0,2,1:T(8,128)(2,1)S(1)}, u32[]{:S(2)}) %copy-start.4) | copy-done | bytes 4194328
  106.1 2.0 fusion.125
  108.1 2.8 copy.50
  110.9 1.4 collective-permute-start.2
  112.3 2.4 copy.51
  116.0 3.0 copy.52
  120.1 4.5 copy.53
  124.7 30.3 %fusion.113 = (f32[32]{0:T(128)S(1)}, f32[32]{0:T(128)S(1)}, f32[32,8,256,32]{3,0,2,1:T(8,128)}) fusion(bf16[2,3,3,32,32]{4,3,2,1,0:T(8,128)(2,1)S(1)} %copy-done.13, bf16[32,1,256,32]{3,0,2,1:T(8,128)(2,1)} %copy.53, bf16[32,8,256,32]{3,0,2,1:T(8,128)(2,1)} %copy-done.4, bf16[32,1,256,32]{3,0,2,1:T(8,128)(2,1)S(1)} %copy.52), kind=kOutput, calls=%fused_computation.201 | convolution fusion | flops 1226833920 | bytes 15278336 | tf_op jit(solution)/shard_map/conv_general_dilated | solution.py:19
  155.0 13.1 %psum.85 = f32[2,32]{1,0:T(2,128)S(1)} all-reduce(f32[2,32]{1,0:T(2,128)S(1)} %pad_maximum_fusion.5), channel_id=1, replica_groups=mesh['dp'=2,'sp'=4] {'sp'}, use_global_device_ids=true, to_apply=%region_5.6 | all-reduce | flops 64 | bytes 512 | tf_op jit(solution)/shard_map/psum | solution.py:32
  168.1 13.7 %maximum_convert_fusion = bf16[32,8,256,32]{3,0,2,1:T(8,128)(2,1)S(1)} fusion(f32[32,8,256,32]{3,0,2,1:T(8,128)} %get-tuple-element.51, f32[32]{0:T(128)S(1)} %get-tuple-element.48, f32[32]{0:T(128)S(1)} %fusion.104, f32[32]{0:T(128)S(1)} %slice_bitcast_fusion.21), kind=kLoop, calls=%fused_computation | loop fusion | flops 10485760 | bytes 12583296 | tf_op jit(solution)/shard_map/convert_element_type | solution.py:39
  181.8 5.7 %copy-done.5 = bf16[32,8,256,32]{3,0,2,1:T(8,128)(2,1)} copy-done((bf16[32,8,256,32]{3,0,2,1:T(8,128)(2,1)}, bf16[32,8,256,32]{3,0,2,1:T(8,128)(2,1)S(1)}, u32[]{:S(2)}) %copy-start.5) | copy-done | bytes 4194328
  187.9 1.7 copy.54
  190.9 2.5 collective-permute-done.4
  193.4 3.0 copy.55
  196.4 16.5 %fusion.121 = (f32[128]{0:T(128)S(1)}, f32[128]{0:T(128)S(1)}, f32[32,4,128,128]{3,0,2,1:T(8,128)}) fusion(bf16[3,3,32,128]{3,2,1,0:T(8,128)(2,1)S(1)} %copy-done, bf16[32,1,256,32]{3,0,2,1:T(8,128)(2,1)S(1)} %copy.55, bf16[32,8,256,32]{3,0,2,1:T(8,128)(2,1)} %copy-done.5), kind=kOutput, calls=%fused_computation.209 | convolution fusion | flops 1220542208 | bytes 13181952 | tf_op jit(solution)/shard_map/conv_general_dilated | solution.py:24
  213.0 12.8 %psum.86 = f32[2,128]{1,0:T(2,128)S(1)} all-reduce(f32[2,128]{1,0:T(2,128)S(1)} %pad_maximum_fusion.6), channel_id=1, replica_groups=mesh['dp'=2,'sp'=4] {'sp'}, use_global_device_ids=true, to_apply=%region_8.9 | all-reduce | flops 256 | bytes 2048 | tf_op jit(solution)/shard_map/psum | solution.py:32
  225.8 4.8 maximum_convert_fusion.2
  230.6 6.8 %fusion.124 = (f32[64]{0:T(128)S(1)}, f32[64]{0:T(128)S(1)}, f32[32,4,128,64]{2,3,1,0:T(8,128)}) fusion(bf16[3,128,64]{1,2,0:T(8,128)(2,1)S(1)} %copy-done.6, bf16[32,4,128,128]{3,0,2,1:T(8,128)(2,1)S(1)} %maximum_convert_fusion.2), kind=kOutput, calls=%fused_computation.212 | convolution fusion | flops 271581056 | bytes 8405504 | tf_op jit(solution)/shard_map/bhwc,cd->bhwd/dot_general | solution.py:27
  237.4 5.7 %psum.87 = f32[2,64]{1,0:T(2,128)S(1)} all-reduce(f32[2,64]{1,0:T(2,128)S(1)} %pad_maximum_fusion.7), channel_id=1, replica_groups=mesh['dp'=2,'sp'=4] {'sp'}, use_global_device_ids=true, to_apply=%region_11.12 | all-reduce | flops 128 | bytes 1024 | tf_op jit(solution)/shard_map/psum | solution.py:32
  243.1 3.1 maximum_convert_fusion.8
  246.3 1.8 collective-permute-start.5
  248.1 1.5 collective-permute-start.6
  249.6 3.7 collective-permute-done.6
  253.8 9.1 %copy.57 = bf16[32,6,128,64]{3,0,2,1:T(8,128)(2,1)} copy(bf16[32,6,128,64]{2,3,1,0:T(8,128)(2,1)S(1)} %pad_maximum_fusion.1) | data formatting | bytes 6291456 | tf_op jit(solution)/shard_map/concatenate | solution.py:18
  262.9 11.7 %fusion.120 = (f32[64]{0:T(128)S(1)}, f32[64]{0:T(128)S(1)}, f32[32,4,128,64]{3,0,2,1:T(8,128)}) fusion(bf16[32,6,128,64]{3,0,2,1:T(8,128)(2,1)} %copy.57, bf16[3,3,3,64,64]{4,3,2,1,0:T(8,128)(2,1)} %param.18), kind=kOutput, calls=%fused_computation.208 | convolution fusion | flops 1204813824 | bytes 10633728 | tf_op jit(solution)/shard_map/conv_general_dilated | solution.py:19
  274.6 12.8 %psum.88 = f32[2,64]{1,0:T(2,128)S(1)} all-reduce(f32[2,64]{1,0:T(2,128)S(1)} %pad_maximum_fusion.8), channel_id=1, replica_groups=mesh['dp'=2,'sp'=4] {'sp'}, use_global_device_ids=true, to_apply=%region_14.15 | all-reduce | flops 128 | bytes 1024 | tf_op jit(solution)/shard_map/psum | solution.py:32
  287.5 6.8 %copy.58 = f32[32,4,128,64]{2,3,1,0:T(8,128)} copy(f32[32,4,128,64]{3,0,2,1:T(8,128)} %get-tuple-element.54) | data formatting | bytes 8388608 | tf_op jit(solution)/shard_map/conv_general_dilated | solution.py:19
  294.3 7.8 %fusion.119 = (f32[128]{0:T(128)S(1)}, f32[128]{0:T(128)S(1)}, f32[32,4,128,128]{3,2,1,0:T(8,128)}) fusion(bf16[3,64,128]{2,1,0:T(8,128)(2,1)S(1)} %copy-done.7, f32[32,4,128,64]{2,3,1,0:T(8,128)} %copy.58, f32[64]{0:T(128)S(1)} %get-tuple-element.44, f32[64]{0:T(128)S(1)} %fusion.95, f32[64]{0:T(128)S(1)} %slice_bitcast_fusion.15), kind=kOutput, calls=%fused_computation.207 | convolution fusion | flops 279969536 | bytes 12601856 | tf_op jit(solution)/shard_map/bhwc,cd->bhwd/dot_general | solution.py:27
  302.1 5.9 %psum.89 = f32[2,128]{1,0:T(2,128)S(1)} all-reduce(f32[2,128]{1,0:T(2,128)S(1)} %pad_maximum_fusion.9), channel_id=1, replica_groups=mesh['dp'=2,'sp'=4] {'sp'}, use_global_device_ids=true, to_apply=%region_17.18 | all-reduce | flops 256 | bytes 2048 | tf_op jit(solution)/shard_map/psum | solution.py:32
  308.0 10.4 %fusion.24 = bf16[32,4,128,128]{3,0,2,1:T(8,128)(2,1)S(1)} fusion(f32[32,4,128,128]{3,2,1,0:T(8,128)} %get-tuple-element.55, f32[128]{0:T(128)S(1)} %get-tuple-element.41, f32[128]{0:T(128)S(1)} %fusion.92, f32[128]{0:T(128)S(1)} %slice_bitcast_fusion.13, f32[128]{0:T(128)S(1)} %slice_bitcast_fusion.18, f32[128]{0:T(128)S(1)} %fusion.101, ...), kind=kLoop, calls=%fused_computation.31 | loop fusion | flops 25165824 | bytes 20974592 | tf_op jit(solution)/shard_map/convert_element_type | solution.py:50
  318.4 2.0 copy-done.3
  320.4 6.8 %fusion.123 = (f32[64]{0:T(128)S(1)}, f32[64]{0:T(128)S(1)}, f32[32,4,128,64]{2,3,1,0:T(8,128)}) fusion(bf16[3,128,64]{1,2,0:T(8,128)(2,1)S(1)} %copy-done.6, bf16[32,4,128,128]{3,0,2,1:T(8,128)(2,1)S(1)} %fusion.24), kind=kOutput, calls=%fused_computation.211 | convolution fusion | flops 271581056 | bytes 8405504 | tf_op jit(solution)/shard_map/bhwc,cd->bhwd/dot_general | solution.py:27
  327.1 6.8 %psum.90 = f32[2,64]{1,0:T(2,128)S(1)} all-reduce(f32[2,64]{1,0:T(2,128)S(1)} %pad_maximum_fusion.10), channel_id=1, replica_groups=mesh['dp'=2,'sp'=4] {'sp'}, use_global_device_ids=true, to_apply=%region_20.21 | all-reduce | flops 128 | bytes 1024 | tf_op jit(solution)/shard_map/psum | solution.py:32
  333.9 3.1 maximum_convert_fusion.6
  337.1 1.3 collective-permute-start.7
  338.4 1.7 collective-permute-start.8
  340.2 3.0 collective-permute-done.8
  343.6 9.1 %copy.61 = bf16[32,6,128,64]{3,0,2,1:T(8,128)(2,1)} copy(bf16[32,6,128,64]{2,3,1,0:T(8,128)(2,1)S(1)} %pad_maximum_fusion.2) | data formatting | bytes 6291456 | tf_op jit(solution)/shard_map/concatenate | solution.py:18
  352.7 11.7 %fusion.118 = (f32[64]{0:T(128)S(1)}, f32[64]{0:T(128)S(1)}, f32[32,4,128,64]{3,0,2,1:T(8,128)}) fusion(bf16[32,6,128,64]{3,0,2,1:T(8,128)(2,1)} %copy.61, bf16[3,3,3,64,64]{4,3,2,1,0:T(8,128)(2,1)} %param.18), kind=kOutput, calls=%fused_computation.206 | convolution fusion | flops 1204813824 | bytes 10633728 | tf_op jit(solution)/shard_map/conv_general_dilated | solution.py:19
  364.4 12.9 %psum.91 = f32[2,64]{1,0:T(2,128)S(1)} all-reduce(f32[2,64]{1,0:T(2,128)S(1)} %pad_maximum_fusion.11), channel_id=1, replica_groups=mesh['dp'=2,'sp'=4] {'sp'}, use_global_device_ids=true, to_apply=%region_23.24 | all-reduce | flops 128 | bytes 1024 | tf_op jit(solution)/shard_map/psum | solution.py:32
  377.2 6.8 %copy.62 = f32[32,4,128,64]{2,3,1,0:T(8,128)} copy(f32[32,4,128,64]{3,0,2,1:T(8,128)} %get-tuple-element.57) | data formatting | bytes 8388608 | tf_op jit(solution)/shard_map/conv_general_dilated | solution.py:19
  384.1 7.8 %fusion.117 = (f32[128]{0:T(128)S(1)}, f32[128]{0:T(128)S(1)}, f32[32,4,128,128]{3,2,1,0:T(8,128)}) fusion(bf16[3,64,128]{2,1,0:T(8,128)(2,1)S(1)} %copy-done.7, f32[32,4,128,64]{2,3,1,0:T(8,128)} %copy.62, f32[64]{0:T(128)S(1)} %get-tuple-element.43, f32[64]{0:T(128)S(1)} %fusion.86, f32[64]{0:T(128)S(1)} %slice_bitcast_fusion.9), kind=kOutput, calls=%fused_computation.205 | convolution fusion | flops 279969536 | bytes 12601856 | tf_op jit(solution)/shard_map/bhwc,cd->bhwd/dot_general | solution.py:27
  391.9 5.8 %psum.92 = f32[2,128]{1,0:T(2,128)S(1)} all-reduce(f32[2,128]{1,0:T(2,128)S(1)} %pad_maximum_fusion.12), channel_id=1, replica_groups=mesh['dp'=2,'sp'=4] {'sp'}, use_global_device_ids=true, to_apply=%region_26.27 | all-reduce | flops 256 | bytes 2048 | tf_op jit(solution)/shard_map/psum | solution.py:32
  397.8 9.6 %fusion.19 = bf16[32,4,128,128]{3,0,2,1:T(8,128)(2,1)S(1)} fusion(f32[32,4,128,128]{3,2,1,0:T(8,128)} %get-tuple-element.58, bf16[32,4,128,128]{3,0,2,1:T(8,128)(2,1)} %copy-done.3, f32[128]{0:T(128)S(1)} %get-tuple-element.40, f32[128]{0:T(128)S(1)} %fusion.83, f32[128]{0:T(128)S(1)} %slice_bitcast_fusion.7), kind=kLoop, calls=%fused_computation.25 | loop fusion | flops 14680064 | bytes 16778752 | tf_op jit(solution)/shard_map/convert_element_type | solution.py:50
  407.4 2.0 copy-done.2
  409.3 6.8 %fusion.122 = (f32[64]{0:T(128)S(1)}, f32[64]{0:T(128)S(1)}, f32[32,4,128,64]{2,3,1,0:T(8,128)}) fusion(bf16[3,128,64]{1,2,0:T(8,128)(2,1)S(1)} %copy-done.6, bf16[32,4,128,128]{3,0,2,1:T(8,128)(2,1)S(1)} %fusion.19), kind=kOutput, calls=%fused_computation.210 | convolution fusion | flops 271581056 | bytes 8405504 | tf_op jit(solution)/shard_map/bhwc,cd->bhwd/dot_general | solution.py:27
  416.1 6.8 %psum.93 = f32[2,64]{1,0:T(2,128)S(1)} all-reduce(f32[2,64]{1,0:T(2,128)S(1)} %pad_maximum_fusion.13), channel_id=1, replica_groups=mesh['dp'=2,'sp'=4] {'sp'}, use_global_device_ids=true, to_apply=%region_29.30 | all-reduce | flops 128 | bytes 1024 | tf_op jit(solution)/shard_map/psum | solution.py:32
  422.9 3.1 maximum_convert_fusion.4
  427.4 3.3 collective-permute-start.9
  432.3 9.1 %copy.65 = bf16[32,6,128,64]{3,0,2,1:T(8,128)(2,1)} copy(bf16[32,6,128,64]{2,3,1,0:T(8,128)(2,1)S(1)} %pad_maximum_fusion.3) | data formatting | bytes 6291456 | tf_op jit(solution)/shard_map/concatenate | solution.py:18
  441.4 11.7 %fusion.116 = (f32[64]{0:T(128)S(1)}, f32[64]{0:T(128)S(1)}, f32[32,4,128,64]{3,0,2,1:T(8,128)}) fusion(bf16[32,6,128,64]{3,0,2,1:T(8,128)(2,1)} %copy.65, bf16[3,3,3,64,64]{4,3,2,1,0:T(8,128)(2,1)} %param.18), kind=kOutput, calls=%fused_computation.204 | convolution fusion | flops 1204813824 | bytes 10633728 | tf_op jit(solution)/shard_map/conv_general_dilated | solution.py:19
  453.1 10.9 %psum.94 = f32[2,64]{1,0:T(2,128)S(1)} all-reduce(f32[2,64]{1,0:T(2,128)S(1)} %pad_maximum_fusion.14), channel_id=1, replica_groups=mesh['dp'=2,'sp'=4] {'sp'}, use_global_device_ids=true, to_apply=%region_32.33 | all-reduce | flops 128 | bytes 1024 | tf_op jit(solution)/shard_map/psum | solution.py:32
  464.0 6.8 %copy.66 = f32[32,4,128,64]{2,3,1,0:T(8,128)} copy(f32[32,4,128,64]{3,0,2,1:T(8,128)} %get-tuple-element.60) | data formatting | bytes 8388608 | tf_op jit(solution)/shard_map/conv_general_dilated | solution.py:19
  470.8 7.8 %fusion.115 = (f32[128]{0:T(128)S(1)}, f32[128]{0:T(128)S(1)}, f32[32,4,128,128]{3,2,1,0:T(8,128)}) fusion(bf16[3,64,128]{2,1,0:T(8,128)(2,1)S(1)} %copy-done.7, f32[32,4,128,64]{2,3,1,0:T(8,128)} %copy.66, f32[64]{0:T(128)S(1)} %get-tuple-element.42, f32[64]{0:T(128)S(1)} %fusion.77, f32[64]{0:T(128)S(1)} %slice_bitcast_fusion.3), kind=kOutput, calls=%fused_computation.203 | convolution fusion | flops 279969536 | bytes 12601856 | tf_op jit(solution)/shard_map/bhwc,cd->bhwd/dot_general | solution.py:27
  478.7 7.5 %psum.95 = f32[2,128]{1,0:T(2,128)S(1)} all-reduce(f32[2,128]{1,0:T(2,128)S(1)} %pad_maximum_fusion.15), channel_id=1, replica_groups=mesh['dp'=2,'sp'=4] {'sp'}, use_global_device_ids=true, to_apply=%region_35.36 | all-reduce | flops 256 | bytes 2048 | tf_op jit(solution)/shard_map/psum | solution.py:32
  486.2 9.6 %fusion.14 = bf16[32,4,128,128]{3,0,2,1:T(8,128)(2,1)S(1)} fusion(f32[32,4,128,128]{3,2,1,0:T(8,128)} %get-tuple-element.61, bf16[32,4,128,128]{3,0,2,1:T(8,128)(2,1)} %copy-done.2, f32[128]{0:T(128)S(1)} %get-tuple-element.39, f32[128]{0:T(128)S(1)} %fusion.74, f32[128]{0:T(128)S(1)} %slice_bitcast_fusion.1), kind=kLoop, calls=%fused_computation.19 | loop fusion | flops 14680064 | bytes 16778752 | tf_op jit(solution)/shard_map/convert_element_type | solution.py:50
  495.8 3.6 copy.68
  (96 shorter events, 11.8 us)
Async XLA Ops:
  0.0 196.4 %copy-start = (bf16[3,3,32,128]{3,2,1,0:T(8,128)(2,1)S(1)}, bf16[3,3,32,128]{3,2,1,0:T(8,128)(2,1)}, u32[]{:S(2)}) copy-start(bf16[3,3,32,128]{3,2,1,0:T(8,128)(2,1)} %param.14) | copy-start | bytes 221188
  1.3 4.8 collective-permute-start
  4.1 5.9 %collective-permute-start.1 = (bf16[32,1,256,32]{2,3,1,0:T(8,128)(2,1)S(1)}, bf16[32,1,256,32]{2,3,1,0:T(8,128)(2,1)S(1)}, u32[]{:S(2)}, u32[]{:S(2)}) collective-permute-start(bf16[32,1,256,32]{2,3,1,0:T(8,128)(2,1)S(1)} %get-tuple-element.32), channel_id=1, source_target_pairs={{1,0},{2,1},{3,2},{5,4},{6,5},{7,6}} | collective-permute-start | bytes 1572872 | tf_op jit(solution)/shard_map/ppermute | solution.py:17
  15.1 28.5 %copy-start.13 = (bf16[2,3,3,32,32]{4,3,2,1,0:T(8,128)(2,1)S(1)}, bf16[2,3,3,32,32]{4,3,2,1,0:T(8,128)(2,1)}, u32[]{:S(2)}) copy-start(bf16[2,3,3,32,32]{4,3,2,1,0:T(8,128)(2,1)} %param.12) | copy-start | bytes 110596
  43.7 43.0 %copy-start.11 = (f32[2,2,32]{2,1,0:T(2,128)S(1)}, f32[2,2,32]{2,1,0:T(2,128)}, u32[]{:S(2)}) copy-start(f32[2,2,32]{2,1,0:T(2,128)} %param.13) | copy-start | bytes 1540
  100.4 5.7 %copy-start.4 = (bf16[32,8,256,32]{3,0,2,1:T(8,128)(2,1)}, bf16[32,8,256,32]{3,0,2,1:T(8,128)(2,1)S(1)}, u32[]{:S(2)}) copy-start(bf16[32,8,256,32]{3,0,2,1:T(8,128)(2,1)S(1)} %maximum_convert_fusion.1) | copy-start | bytes 12582916
  110.9 5.1 %collective-permute-start.2 = (bf16[32,1,256,32]{2,3,1,0:T(8,128)(2,1)S(1)}, bf16[32,1,256,32]{2,3,1,0:T(8,128)(2,1)S(1)}, u32[]{:S(2)}, u32[]{:S(2)}) collective-permute-start(bf16[32,1,256,32]{2,3,1,0:T(8,128)(2,1)S(1)} %copy.50), channel_id=1, source_target_pairs={{0,1},{1,2},{2,3},{4,5},{5,6},{6,7}} | collective-permute-start | bytes 1572872 | tf_op jit(solution)/shard_map/ppermute | solution.py:16
  114.7 5.5 %collective-permute-start.3 = (bf16[32,1,256,32]{2,3,1,0:T(8,128)(2,1)}, bf16[32,1,256,32]{2,3,1,0:T(8,128)(2,1)}, u32[]{:S(2)}, u32[]{:S(2)}) collective-permute-start(bf16[32,1,256,32]{2,3,1,0:T(8,128)(2,1)} %copy.51), channel_id=1, source_target_pairs={{1,0},{2,1},{3,2},{5,4},{6,5},{7,6}} | collective-permute-start | bytes 1572872 | tf_op jit(solution)/shard_map/ppermute | solution.py:17
  181.8 5.7 %copy-start.5 = (bf16[32,8,256,32]{3,0,2,1:T(8,128)(2,1)}, bf16[32,8,256,32]{3,0,2,1:T(8,128)(2,1)S(1)}, u32[]{:S(2)}) copy-start(bf16[32,8,256,32]{3,0,2,1:T(8,128)(2,1)S(1)} %maximum_convert_fusion) | copy-start | bytes 12582916
  187.5 3.4 copy-start.12
  187.5 3.4 copy-start.8
  189.6 3.8 collective-permute-start.4
  225.7 4.9 copy-start.6
  237.4 12.2 %copy-start.9 = (f32[3,2,64]{2,1,0:T(2,128)S(1)}, f32[3,2,64]{2,1,0:T(2,128)}, u32[]{:S(2)}) copy-start(f32[3,2,64]{2,1,0:T(2,128)} %param.19) | copy-start | bytes 4612
  237.4 12.2 %copy-start.10 = (f32[3,2,128]{2,1,0:T(2,128)S(1)}, f32[3,2,128]{2,1,0:T(2,128)}, u32[]{:S(2)}) copy-start(f32[3,2,128]{2,1,0:T(2,128)} %param.21) | copy-start | bytes 9220
  246.3 3.3 collective-permute-start.5
  248.1 5.3 %collective-permute-start.6 = (bf16[32,1,128,64]{2,3,1,0:T(8,128)(2,1)S(1)}, bf16[32,1,128,64]{2,3,1,0:T(8,128)(2,1)S(1)}, u32[]{:S(2)}, u32[]{:S(2)}) collective-permute-start(bf16[32,1,128,64]{2,3,1,0:T(8,128)(2,1)S(1)} %get-tuple-element.38), channel_id=1, source_target_pairs={{1,0},{2,1},{3,2},{5,4},{6,5},{7,6}} | collective-permute-start | bytes 1572872 | tf_op jit(solution)/shard_map/ppermute | solution.py:17
  287.4 6.8 %copy-start.7 = (bf16[3,64,128]{2,1,0:T(8,128)(2,1)S(1)}, bf16[3,64,128]{2,1,0:T(8,128)(2,1)}, u32[]{:S(2)}) copy-start(bf16[3,64,128]{2,1,0:T(8,128)(2,1)} %param.20) | copy-start | bytes 147460
  318.4 2.0 copy-start.3
  337.1 3.0 collective-permute-start.7
  338.4 4.8 collective-permute-start.8
  407.3 2.0 copy-start.2
  426.1 4.6 collective-permute-start.10
  427.4 4.6 collective-permute-start.9
  486.2 13.3 %copy-start.1 = (bf16[3,3,32,128]{3,2,1,0:T(8,128)(2,1)S(1)}, bf16[3,3,32,128]{3,2,1,0:T(8,128)(2,1)}, u32[]{:S(2)}) copy-start(bf16[3,3,32,128]{3,2,1,0:T(8,128)(2,1)} %param.14) | copy-start | bytes 221188
where the time goes:
time: 508 us; the launch traced here: 500 us
  matrix products  156 us (31%)
  local copies, waits for them, and re-layouts  117 us (23%)
  blocking collectives  114 us (22%)
  other arithmetic  77.6 us (15%)
  starting transfers between devices  18.9 us (4%)
  waiting for transfers between devices  15.6 us (3%)
    psum x12, blocking collectives, batch_norm(): group_moments = lax.psum(part_sums, 'sp') / norm_count  114 us
    conv_general_dilated x5, matrix products, conv_same(): lax.conv_general_dilated(padded, weight, (1, 1), ((0, 0), (1, 1)), dimens...  95.3 us
    concatenate x4, local copies, waits for them, and re-layouts, conv_same(): padded = jnp.concatenate([from_above, hidden, from_below], axis=1)  55.8 us
    dot_general x6, matrix products, conv_point(): jnp.einsum('bhwc,cd->bhwd', hidden, weight, preferred_element_type=jnp.fl...  43.8 us
    convert_element_type x6, other arithmetic, norm_relu(): return jax.nn.relu(batch_norm(pre_act, params)).astype(jnp.bfloat16)  41.4 us
    convert_element_type x3, other arithmetic, forward(): hidden = jax.nn.relu(summed).astype(jnp.bfloat16)  29.6 us
    conv_general_dilated x3, local copies, waits for them, and re-layouts, conv_same(): lax.conv_general_dilated(padded, weight, (1, 1), ((0, 0), (1, 1)), dimens...  20.4 us
    conv_general_dilated x1, matrix products, conv_down(): lax.conv_general_dilated(padded, weight, (2, 2), ((0, 0), (0, 1)), dimens...  16.5 us
  transfers between devices with their start and end apart: 11, of which 6 were waited for; matrix products, arithmetic and copies ran while one was open for 1% of the time, Pallas kernels for 0%

commit v1 on v0

v1 whole, which is shorter than its diff:
```python
import jax
import jax.numpy as jnp
from jax import lax
from jax.experimental import pallas as pl
from jax.experimental.pallas import tpu as pltpu
from jax.sharding import PartitionSpec as P

NORM_EPS = 1e-5
MESH = pl.DeviceIdType.MESH
F32 = jnp.float32
BF16 = jnp.bfloat16
ROWS_A = 8
ROWS_B = 4
LANES = 256


def band(weight, taps_h, taps_w, phases):
    kernel = jnp.transpose(weight, (3, 0, 1, 2))
    free_h, free_w = taps_h - 3, taps_w - 3
    blocks = []
    for row in range(free_h + 1):
        for phase in phases:
            blocks.append(jnp.pad(kernel, ((0, 0), (row, free_h - row), (phase, free_w - phase), (0, 0))))
    out = jnp.concatenate(blocks, axis=0)
    return out.reshape(out.shape[0], taps_h * taps_w * weight.shape[2])


def solution(mesh):
    groups = mesh.shape["sp"]

    def kernel(x_hbm, wa, wd, wi, wm, wo, bn, out_hbm,
               xv, xh, hs, us, za, zb, hb, ov, acc, ab, stat,
               x_sem, out_sem, halo_send, halo_recv, stat_send, stat_recv):
        pairs = xv.shape[0]
        me = lax.axis_index("sp")
        count_a = float(2 * pairs * ROWS_A * LANES * groups)
        count_b = float(2 * pairs * ROWS_B * 128 * groups)

        def x_copy(pair):
            return pltpu.make_async_copy(x_hbm.at[pl.ds(2 * pair, 2)], xv.at[pair], x_sem.at[pair])

        @pl.loop(0, pairs)
        def _(pair):
            x_copy(pair).start()

        barrier = pltpu.get_barrier_semaphore()
        for hop in range(1, groups):
            pl.semaphore_signal(barrier, inc=1, device_id={"sp": lax.rem(me + hop, groups)}, device_id_type=MESH)
        pl.semaphore_wait(barrier, groups - 1)

        def halo_copy(step, side, src, dst):
            peer = me + 1 if side == 0 else me - 1
            return pltpu.make_async_remote_copy(
                src_ref=src, dst_ref=dst, send_sem=halo_send.at[step, side], recv_sem=halo_recv.at[step, side],
                device_id={"sp": peer}, device_id_type=MESH)

        def has_peer(side):
            return me < groups - 1 if side == 0 else me > 0

        def from_peer(side):
            return me > 0 if side == 0 else me < groups - 1

        def exchange(step, side, src, dst):
            @pl.when(has_peer(side))
            def _():
                halo_copy(step, side, src, dst).start()

        def settle(step, side, src, dst):
            @pl.when(from_peer(side))
            def _():
                pltpu.make_async_remote_copy(
                    src_ref=src, dst_ref=dst, send_sem=halo_send.at[step, side], recv_sem=halo_recv.at[step, side],
                    device_id={"sp": me}, device_id_type=MESH).wait_recv()

            @pl.when(has_peer(side))
            def _():
                halo_copy(step, side, src, dst).wait_send()

        x_src = (x_hbm.at[:, ROWS_A - 1], x_hbm.at[:, 0])
        x_dst = (xh.at[0], xh.at[1])
        for side in range(2):
            exchange(0, side, x_src[side], x_dst[side])

        @pl.when(me == 0)
        def _():
            xh[0] = jnp.zeros(xh.shape[1:], BF16)

            @pl.loop(0, pairs)
            def _(pair):
                hs[pair, 0] = jnp.zeros(hs.shape[2:], BF16)
                us[pair, 0] = jnp.zeros(us.shape[2:], BF16)

        @pl.when(me == groups - 1)
        def _():
            xh[1] = jnp.zeros(xh.shape[1:], BF16)

            @pl.loop(0, pairs)
            def _(pair):
                hs[pair, ROWS_A + 1] = jnp.zeros(hs.shape[2:], BF16)
                us[pair, ROWS_B + 1] = jnp.zeros(us.shape[2:], BF16)

        def shift(value, step):
            lane = lax.broadcasted_iota(jnp.int32, (value.shape[0], 128), 1)
            edge = 0 if step == 1 else 127
            halves = []
            for half in range(2):
                moved = pltpu.roll(value[:, half * 128:(half + 1) * 128], step % 128, 1)
                halves.append(jnp.where(lane == edge, 0.0, moved))
            return jnp.concatenate(halves, axis=1)

        def put_planes(pair, row, even, odd, centre=True):
            hs[pair, row, 0:32] = shift(odd, 1).astype(BF16)
            if centre:
                hs[pair, row, 32:64] = even.astype(BF16)
                hs[pair, row, 64:96] = odd.astype(BF16)
            hs[pair, row, 96:128] = shift(even, -1).astype(BF16)

        def put_mid(pair, row, value, centre=True):
            us[pair, row, 0:64] = shift(value, 1).astype(BF16)
            if centre:
                us[pair, row, 64:128] = value.astype(BF16)
            us[pair, row, 128:192] = shift(value, -1).astype(BF16)

        def rebuild_a(pair, row):
            both = hs[pair, row, 32:96].astype(F32)
            put_planes(pair, row, both[0:32], both[32:64], centre=False)

        def rebuild_mid(pair, row):
            put_mid(pair, row, us[pair, row, 64:128].astype(F32), centre=False)

        def clear():
            acc[...] = jnp.zeros(acc.shape, F32)

        def tally(value):
            left, right = value[:, :128], value[:, 128:]
            rows = value.shape[0]
            acc[0, 0:rows] += left + right
            acc[1, 0:rows] += left * left + right * right

        def moments(layer, channels, count):
            for part in range(2):
                turned = acc[part].T.reshape(16, 8, 128)
                stat[layer, me, 8 * part:8 * part + 8] = jnp.sum(turned, axis=0)
            copies = []
            for hop in range(1, groups):
                copies.append(pltpu.make_async_remote_copy(
                    src_ref=stat.at[layer, me], dst_ref=stat.at[layer, me],
                    send_sem=stat_send.at[layer, hop], recv_sem=stat_recv.at[layer, hop],
                    device_id={"sp": lax.rem(me + hop, groups)}, device_id_type=MESH))
            for copy in copies:
                copy.start()
            for hop in range(1, groups):
                origin = lax.rem(me + groups - hop, groups)
                pltpu.make_async_remote_copy(
                    src_ref=stat.at[layer, origin], dst_ref=stat.at[layer, origin],
                    send_sem=stat_send.at[layer, hop], recv_sem=stat_recv.at[layer, hop],
                    device_id={"sp": origin}, device_id_type=MESH).wait_recv()
            for copy in copies:
                copy.wait_send()
            total = stat[layer, 0]
            for origin in range(1, groups):
                total = total + stat[layer, origin]

            def fold(block):
                line = jnp.broadcast_to(jnp.sum(block, axis=0, keepdims=True), (8, 128))
                width = 64
                while width >= channels:
                    line = line + pltpu.roll(line, width, 1)
                    width //= 2
                return line / count

            mean, square = fold(total[0:8]), fold(total[8:16])
            var = square - mean * mean
            scale = bn[layer, 0:1] * lax.rsqrt(var + NORM_EPS)
            bias = bn[layer, 1:2] - mean * scale
            ab[0] = jnp.broadcast_to(scale[0:1], (128, 128)).T
            ab[1] = jnp.broadcast_to(bias[0:1], (128, 128)).T
            clear()

        def affine(value):
            rows = value.shape[0]
            scale, bias = ab[0, 0:rows], ab[1, 0:rows]
            return jnp.concatenate(
                [value[:, :128] * scale + bias, value[:, 128:] * scale + bias], axis=1)

        def norm_relu(value):
            return jnp.maximum(affine(value), 0.0)

        def mm(left, right):
            return jnp.dot(left, right, preferred_element_type=F32)

        clear()

        lane_in = lax.broadcasted_iota(jnp.int32, (LANES, LANES), 0)
        lane_out = lax.broadcasted_iota(jnp.int32, (LANES, LANES), 1)
        source = jnp.where(lane_out < 128, 2 * lane_out, 2 * lane_out - (LANES - 1))
        perm = jnp.where(lane_in == source, 1.0, 0.0).astype(BF16)

        def split_rows(first, second, pair, row):
            one, two = mm(first, perm), mm(second, perm)
            put_planes(pair, row, jnp.concatenate([one[:, :128], two[:, :128]], axis=1),
                       jnp.concatenate([one[:, 128:], two[:, 128:]], axis=1))

        def conv_a(layer, pair, row, rows):
            window = hs[pair, row:row + rows + 2].reshape((rows + 2) * 128, LANES)
            value = mm(wa[layer, 0:64 * rows, 0:128 * (rows + 2)], window)
            tally(value)
            za[pl.ds(pair * ROWS_A + row, rows)] = value.reshape(rows, 64, LANES)

        def norm_a(pair, row):
            value = norm_relu(za[pair * ROWS_A + row])
            put_planes(pair, row + 1, value[0:32], value[32:64])

        @pl.loop(0, pairs)
        def _(pair):
            x_copy(pair).wait()
            for row in range(ROWS_A):
                split_rows(xv[pair, 0, row], xv[pair, 1, row], pair, row + 1)
            for row in range(1, ROWS_A - 1, 2):
                conv_a(0, pair, row, 2)

        for side in range(2):
            settle(0, side, x_src[side], x_dst[side])

        @pl.loop(0, pairs)
        def _(pair):
            split_rows(xh[0, 2 * pair], xh[0, 2 * pair + 1], pair, 0)
            split_rows(xh[1, 2 * pair], xh[1, 2 * pair + 1], pair, ROWS_A + 1)
            conv_a(0, pair, 0, 1)
            conv_a(0, pair, ROWS_A - 1, 1)

        moments(0, 32, count_a)

        a_src = (hs.at[:, ROWS_A, 32:96], hs.at[:, 1, 32:96])
        a_dst = (hs.at[:, 0, 32:96], hs.at[:, ROWS_A + 1, 32:96])

        @pl.loop(0, pairs)
        def _(pair):
            norm_a(pair, 0)
            norm_a(pair, ROWS_A - 1)

        for side in range(2):
            exchange(1, side, a_src[side], a_dst[side])

        @pl.loop(0, pairs)
        def _(pair):
            for row in range(1, ROWS_A - 1):
                norm_a(pair, row)
            for row in range(1, ROWS_A - 1, 2):
                conv_a(1, pair, row, 2)

        for side in range(2):
            settle(1, side, a_src[side], a_dst[side])

        @pl.loop(0, pairs)
        def _(pair):
            rebuild_a(pair, 0)
            rebuild_a(pair, ROWS_A + 1)
            conv_a(1, pair, 0, 1)
            conv_a(1, pair, ROWS_A - 1, 1)

        moments(1, 32, count_a)

        def conv_down(pair, row):
            window = hs[pair, 2 * row + 1:2 * row + 4].reshape(384, LANES)
            value = mm(wd[...], window)
            tally(value)
            zb[pair * ROWS_B + row] = value

        @pl.loop(0, pairs)
        def _(pair):
            norm_a(pair, 0)

        exchange(2, 1, a_src[1], a_dst[1])

        @pl.loop(0, pairs)
        def _(pair):
            for row in range(1, ROWS_A):
                norm_a(pair, row)
            for row in range(ROWS_B - 1):
                conv_down(pair, row)

        settle(2, 1, a_src[1], a_dst[1])

        @pl.loop(0, pairs)
        def _(pair):
            rebuild_a(pair, ROWS_A + 1)
            conv_down(pair, ROWS_B - 1)

        moments(2, 128, count_b)

        def conv_in(block, index, hidden):
            value = mm(wi[block], hidden)
            tally(value)
            za[index] = value

        def conv_mid(block, pair, row, rows):
            window = us[pair, row:row + rows + 2].reshape((rows + 2) * 192, LANES)
            value = mm(wm[block, 0:64 * rows, 0:192 * (rows + 2)], window)
            tally(value)
            za[pl.ds(pair * ROWS_B + row, rows)] = value.reshape(rows, 64, LANES)

        def norm_mid(pair, row):
            put_mid(pair, row + 1, norm_relu(za[pair * ROWS_B + row]))

        m_src = (us.at[:, ROWS_B, 64:128], us.at[:, 1, 64:128])
        m_dst = (us.at[:, 0, 64:128], us.at[:, ROWS_B + 1, 64:128])

        @pl.loop(0, pairs)
        def _(pair):
            for row in range(ROWS_B):
                index = pair * ROWS_B + row
                hidden = norm_relu(zb[index]).astype(BF16)
                hb[index] = hidden
                conv_in(0, index, hidden)

        blocks = wi.shape[0]
        for block in range(blocks):
            layer, step = 3 + 3 * block, 3 + block
            moments(layer, 64, count_b)

            @pl.loop(0, pairs)
            def _(pair):
                norm_mid(pair, 0)
                norm_mid(pair, ROWS_B - 1)

            for side in range(2):
                exchange(step, side, m_src[side], m_dst[side])

            @pl.loop(0, pairs)
            def _(pair):
                for row in range(1, ROWS_B - 1):
                    norm_mid(pair, row)
                conv_mid(block, pair, 1, 2)

            for side in range(2):
                settle(step, side, m_src[side], m_dst[side])

            @pl.loop(0, pairs)
            def _(pair):
                rebuild_mid(pair, 0)
                rebuild_mid(pair, ROWS_B + 1)
                conv_mid(block, pair, 0, 1)
                conv_mid(block, pair, ROWS_B - 1, 1)

            moments(layer + 1, 64, count_b)

            @pl.loop(0, pairs)
            def _(pair):
                for row in range(ROWS_B):
                    index = pair * ROWS_B + row
                    value = mm(wo[block], norm_relu(za[index]).astype(BF16))
                    tally(value)
                    zb[index] = value

            moments(layer + 2, 128, count_b)

            def finish(index):
                return jnp.maximum(affine(zb[index]) + hb[index].astype(F32), 0.0)

            if block < blocks - 1:
                @pl.loop(0, pairs)
                def _(pair):
                    for row in range(ROWS_B):
                        index = pair * ROWS_B + row
                        hidden = finish(index).astype(BF16)
                        hb[index] = hidden
                        conv_in(block + 1, index, hidden)
            else:
                def out_copy(pair):
                    return pltpu.make_async_copy(ov.at[pair], out_hbm.at[pl.ds(2 * pair, 2)], out_sem.at[pair])

                @pl.loop(0, pairs)
                def _(pair):
                    for row in range(ROWS_B):
                        value = finish(pair * ROWS_B + row)
                        for image in range(2):
                            ov[pair, image, row] = value[:, image * 128:(image + 1) * 128].T.astype(BF16)
                    out_copy(pair).start()

                @pl.loop(0, pairs)
                def _(pair):
                    out_copy(pair).wait()

    def forward(images, w_a, bn_a, w_down, bn_down, w_in, bn_in, w_mid, bn_mid, w_out, bn_out):
        images_count = images.shape[0]
        pairs = images_count // 2
        x = jnp.transpose(images, (0, 1, 3, 2))
        wa = jnp.stack([band(w_a[layer], 4, 4, (0, 1)) for layer in range(w_a.shape[0])])
        wd = band(w_down, 3, 4, (1,))
        wi = jnp.transpose(w_in, (0, 2, 1))
        wm = jnp.stack([band(w_mid[block], 4, 3, (0,)) for block in range(w_mid.shape[0])])
        wo = jnp.transpose(w_out, (0, 2, 1))
        bn = [jnp.tile(bn_a[layer], (1, 4)) for layer in range(w_a.shape[0])] + [bn_down]
        for block in range(w_in.shape[0]):
            bn += [jnp.tile(bn_in[block], (1, 2)), jnp.tile(bn_mid[block], (1, 2)), bn_out[block]]
        bn = jnp.stack(bn)
        layers = bn.shape[0]
        steps = 3 + w_in.shape[0]
        vmem = pl.BlockSpec(memory_space=pltpu.VMEM)
        hbm = pl.BlockSpec(memory_space=pl.ANY)
        dma = pltpu.SemaphoreType.DMA
        return pl.pallas_call(
            kernel,
            out_shape=jax.ShapeDtypeStruct((images_count, ROWS_B, 128, 128), BF16),
            in_specs=[hbm] + [vmem] * 6,
            out_specs=hbm,
            scratch_shapes=[
                pltpu.VMEM((pairs, 2, ROWS_A, 32, LANES), BF16),
                pltpu.VMEM((2, images_count, 32, LANES), BF16),
                pltpu.VMEM((pairs, ROWS_A + 2, 128, LANES), BF16),
                pltpu.VMEM((pairs, ROWS_B + 2, 192, LANES), BF16),
                pltpu.VMEM((pairs * ROWS_A, 64, LANES), F32),
                pltpu.VMEM((pairs * ROWS_B, 128, LANES), F32),
                pltpu.VMEM((pairs * ROWS_B, 128, LANES), BF16),
                pltpu.VMEM((pairs, 2, ROWS_B, 128, 128), BF16),
                pltpu.VMEM((2, 128, 128), F32),
                pltpu.VMEM((2, 128, 128), F32),
                pltpu.VMEM((layers, groups, 16, 128), F32),
                dma((pairs,)), dma((pairs,)), dma((steps, 2)), dma((steps, 2)),
                dma((layers, groups)), dma((layers, groups)),
            ],
            compiler_params=pltpu.CompilerParams(
                collective_id=0, has_side_effects=True, vmem_limit_bytes=67043328),
            name="conv_stack",
        )(x, wa, wd, wi, wm, wo, bn)

    act_spec = P("dp", "sp", None, None)
    return jax.shard_map(forward, mesh=mesh, in_specs=(act_spec,) + (P(),) * 10, out_specs=act_spec, check_vma=False)
```

time: 508 us -> 179 us (0.35); the launches traced: 500 us -> 178 us
  matrix products: 156 us -> 0 us
  Pallas kernels: 0 us -> 153 us
  blocking collectives: 114 us -> 0 us
  local copies, waits for them, and re-layouts: 117 us -> 23 us
  other arithmetic: 77.6 us -> 2.18 us
  starting transfers between devices: 18.9 us -> 0 us
  waiting for transfers between devices: 15.6 us -> 0 us
    pallas_call x0 -> x1, Pallas kernels: none -> 153 us  [forward(): pl.pallas_call(kernel, out_shape=jax.ShapeDtypeStruct((images_count, ROWS...]
    psum x12 -> x0, blocking collectives: 114 us -> none  [batch_norm(): group_moments = lax.psum(part_sums, 'sp') / norm_count]
    conv_general_dilated x6 -> x0, matrix products: 112 us -> none  [the longest x5 95.3 us: conv_same(): lax.conv_general_dilated(padded, weight, (1, 1), ((0, 0), (1, 1)), dimens...]
    convert_element_type x9 -> x0, other arithmetic: 71 us -> none  [the longest x6 41.4 us: norm_relu(): return jax.nn.relu(batch_norm(pre_act, params)).astype(jnp.bfloat16)]
    concatenate x4 -> x0, local copies, waits for them, and re-layouts: 55.8 us -> none  [conv_same(): padded = jnp.concatenate([from_above, hidden, from_below], axis=1)]
    dot_general x6 -> x0, matrix products: 43.8 us -> none  [conv_point(): jnp.einsum('bhwc,cd->bhwd', hidden, weight, preferred_element_type=jnp.fl...]
    conv_general_dilated x3 -> x0, local copies, waits for them, and re-layouts: 20.4 us -> none  [conv_same(): lax.conv_general_dilated(padded, weight, (1, 1), ((0, 0), (1, 1)), dimens...]
    ppermute x11 -> x0, starting transfers between devices: 18.9 us -> none  [the longest x5 10.6 us: conv_same(): from_above = lax.ppermute(hidden[:, -1:], 'sp', to_next)]
  transfers between devices with their start and end apart: 11 -> 0, of which waited for: 6 -> 0; matrix products, arithmetic and copies ran while one was open for 1% -> 0% of each run, Pallas kernels for 0% -> 0%
where the time goes in v1:
time: 179 us; the launch traced here: 178 us
  Pallas kernels  153 us (85%)
  local copies, waits for them, and re-layouts  23 us (13%)
  other arithmetic  2.18 us (1%)
    pallas_call x1, Pallas kernels, forward(): pl.pallas_call(kernel, out_shape=jax.ShapeDtypeStruct((images_count, ROWS...  153 us
    unnamed x13, local copies, waits for them, and re-layouts  14.6 us

profile of v1, /device:TPU:0, one launch (start us, length us, event | category | flops | bytes accessed | tf_op | source)
XLA Modules:
  0.0 178.2 jit_solution(4862724569162038373)
XLA Ops:
  0.0 0.7 slice_bitcast_fusion.11
  0.7 0.1 tile.77
  0.8 0.7 slice_bitcast_fusion.6
  1.5 0.1 tile.92
  1.6 0.1 tile.80
  1.7 0.1 tile.86
  1.8 0.7 slice_bitcast_fusion.5
  2.5 0.1 tile.95
  2.6 0.1 tile.83
  2.7 0.1 tile.89
  2.7 0.1 tile.74
  2.8 0.5 constant_dynamic-update-slice_fusion.11
  3.3 0.6 constant_dynamic-update-slice_fusion.10
  3.9 1.2 constant_dynamic-update-slice_fusion.9
  5.2 0.6 constant_dynamic-update-slice_fusion.8
  5.8 0.6 constant_dynamic-update-slice_fusion.7
  6.3 1.3 constant_dynamic-update-slice_fusion.6
  7.6 0.5 constant_dynamic-update-slice_fusion.5
  8.1 0.6 constant_dynamic-update-slice_fusion.4
  8.7 1.2 constant_dynamic-update-slice_fusion.3
  10.0 0.6 constant_dynamic-update-slice_fusion.2
  10.5 0.6 constant_dynamic-update-slice_fusion.1
  11.1 1.3 constant_dynamic-update-slice_fusion.bn
  12.4 0.9 pad.60
  13.3 0.8 copy.25.wd
  14.0 1.6 copy.24
  15.6 0.9 slice_bitcast_fusion.4
  16.5 0.2 fusion.21
  16.7 0.1 copy.19
  16.9 0.1 copy.20
  17.0 0.7 pad_maximum_fusion.1.wa
  17.7 1.1 slice_bitcast_fusion.2
  18.8 0.2 fusion.16
  19.0 0.1 copy.21
  19.2 0.1 copy.22
  19.3 0.1 fusion.18
  19.4 0.1 copy.23
  19.6 0.9 pad_maximum_fusion.wm
  20.5 152.9 %conv_stack.1 = bf16[32,4,128,128]{3,2,1,0:T(8,128)(2,1)} custom-call(bf16[32,8,32,256]{3,2,1,0:T(8,128)(2,1)} %bitcast.48, bf16[2,128,512]{2,1,0:T(8,128)(2,1)} %pad_maximum_fusion.1.wa, bf16[128,384]{1,0:T(8,128)(2,1)} %copy.25.wd, bf16[3,64,128]{2,1,0:T(8,128)(2,1)} %bitcast.57, bf16[3,128,768]{2,1,0:T(8,128)(2,1)} %pad_maximum_fusion.wm, ...), custom_call_target="tpu_custom_call" | custom-call | tf_op jit(solution)/shard_map/conv_stack/pallas_call | solution.py:403
  173.4 4.8 %copy.38 = bf16[32,4,128,128]{3,2,1,0:T(8,128)(2,1)} copy(bf16[32,4,128,128]{3,2,1,0:T(8,128)(2,1)} %conv_stack.1) | data formatting | bytes 8388608
  (8 shorter events, 0.0 us)

commit v2 on v1

--- a/solution.py
+++ b/solution.py
@@ -11,35 +11,33 @@
 BF16 = jnp.bfloat16
 ROWS_A = 8
 ROWS_B = 4
+UNROLL = 4
 LANES = 256
-
-
-def band(weight, taps_h, taps_w, phases):
-    kernel = jnp.transpose(weight, (3, 0, 1, 2))
-    free_h, free_w = taps_h - 3, taps_w - 3
-    blocks = []
-    for row in range(free_h + 1):
-        for phase in phases:
-            blocks.append(jnp.pad(kernel, ((0, 0), (row, free_h - row), (phase, free_w - phase), (0, 0))))
-    out = jnp.concatenate(blocks, axis=0)
-    return out.reshape(out.shape[0], taps_h * taps_w * weight.shape[2])
 
 
 def solution(mesh):
     groups = mesh.shape["sp"]
 
-    def kernel(x_hbm, wa, wd, wi, wm, wo, bn, out_hbm,
-               xv, xh, hs, us, za, zb, hb, ov, acc, ab, stat,
+    def kernel(x_hbm, raw_a, bn_a, raw_d, bn_d, wi, bn_i, raw_m, bn_m, raw_o, bn_o, out_hbm,
+               wa, wd, wm, wo, xv, xh, hs, us, za, zb, hb, ov, acc, ab, stat,
                x_sem, out_sem, halo_send, halo_recv, stat_send, stat_recv):
         pairs = xv.shape[0]
         me = lax.axis_index("sp")
         count_a = float(2 * pairs * ROWS_A * LANES * groups)
         count_b = float(2 * pairs * ROWS_B * 128 * groups)
 
+        def sweep(body, unroll=UNROLL):
+            @pl.loop(0, pairs // unroll)
+            def _(step):
+                sums = [body(step * unroll + part) for part in range(unroll)]
+                if sums[0] is not None:
+                    channels = sums[0].shape[1]
+                    acc[:, 0:channels] += sum(sums[1:], sums[0])
+
         def x_copy(pair):
             return pltpu.make_async_copy(x_hbm.at[pl.ds(2 * pair, 2)], xv.at[pair], x_sem.at[pair])
 
-        @pl.loop(0, pairs)
+        @sweep
         def _(pair):
             x_copy(pair).start()
 
@@ -85,7 +83,7 @@
         def _():
             xh[0] = jnp.zeros(xh.shape[1:], BF16)
 
-            @pl.loop(0, pairs)
+            @sweep
             def _(pair):
                 hs[pair, 0] = jnp.zeros(hs.shape[2:], BF16)
                 us[pair, 0] = jnp.zeros(us.shape[2:], BF16)
@@ -94,10 +92,45 @@
         def _():
             xh[1] = jnp.zeros(xh.shape[1:], BF16)
 
-            @pl.loop(0, pairs)
+            @sweep
             def _(pair):
                 hs[pair, ROWS_A + 1] = jnp.zeros(hs.shape[2:], BF16)
                 us[pair, ROWS_B + 1] = jnp.zeros(us.shape[2:], BF16)
+
+        def turn(block):
+            return block.astype(F32).T.astype(BF16)
+
+        def prepare_a(layer):
+            for row in range(4):
+                lines = []
+                for plane in range(4):
+                    tiles = []
+                    for out_row in range(2):
+                        for phase in range(2):
+                            high, wide = row - out_row, plane - phase
+                            inside = 0 <= high < 3 and 0 <= wide < 3
+                            tiles.append(raw_a[layer, high, wide].astype(F32) if inside else jnp.zeros((32, 32), F32))
+                    lines.append(jnp.concatenate(tiles, axis=1))
+                wa[layer, :, 128 * row:128 * row + 128] = turn(jnp.concatenate(lines, axis=0))
+
+        def prepare_down():
+            for high in range(3):
+                lines = [jnp.zeros((32, 128), BF16)] + [raw_d[high, wide] for wide in range(3)]
+                wd[:, 128 * high:128 * high + 128] = turn(jnp.concatenate(lines, axis=0))
+
+        def prepare_block(block):
+            lines = []
+            for row in range(4):
+                for wide in range(3):
+                    tiles = []
+                    for out_row in range(2):
+                        high = row - out_row
+                        inside = 0 <= high < 3
+                        tiles.append(raw_m[block, high, wide].astype(F32) if inside else jnp.zeros((64, 64), F32))
+                    lines.append(jnp.concatenate(tiles, axis=1))
+            for part in range(6):
+                wm[block, :, 128 * part:128 * part + 128] = turn(jnp.concatenate(lines[2 * part:2 * part + 2], axis=0))
+            wo[block] = turn(raw_o[block])
 
         def shift(value, step):
             lane = lax.broadcasted_iota(jnp.int32, (value.shape[0], 128), 1)
@@ -131,13 +164,17 @@
         def clear():
             acc[...] = jnp.zeros(acc.shape, F32)
 
-        def tally(value):
-            left, right = value[:, :128], value[:, 128:]
-            rows = value.shape[0]
-            acc[0, 0:rows] += left + right
-            acc[1, 0:rows] += left * left + right * right
-
-        def moments(layer, channels, count):
+        def tally(channels, *values):
+            total, square = 0.0, 0.0
+            for value in values:
+                for half in range(2):
+                    for row in range(0, value.shape[0], channels):
+                        piece = value[row:row + channels, half * 128:(half + 1) * 128]
+                        total, square = total + piece, square + piece * piece
+            return jnp.stack([total, square])
+
+        def moments(layer, params, count, during=None):
+            channels = params.shape[1]
             for part in range(2):
                 turned = acc[part].T.reshape(16, 8, 128)
                 stat[layer, me, 8 * part:8 * part + 8] = jnp.sum(turned, axis=0)
@@ -149,6 +186,9 @@
                     device_id={"sp": lax.rem(me + hop, groups)}, device_id_type=MESH))
             for copy in copies:
                 copy.start()
+            clear()
+            if during is not None:
+                during()
             for hop in range(1, groups):
                 origin = lax.rem(me + groups - hop, groups)
                 pltpu.make_async_remote_copy(
@@ -171,11 +211,11 @@
 
             mean, square = fold(total[0:8]), fold(total[8:16])
             var = square - mean * mean
-            scale = bn[layer, 0:1] * lax.rsqrt(var + NORM_EPS)
-            bias = bn[layer, 1:2] - mean * scale
+            wide = jnp.concatenate([params] * (128 // channels), axis=1)
+            scale = wide[0:1] * lax.rsqrt(var + NORM_EPS)
+            bias = wide[1:2] - mean * scale
             ab[0] = jnp.broadcast_to(scale[0:1], (128, 128)).T
             ab[1] = jnp.broadcast_to(bias[0:1], (128, 128)).T
-            clear()
 
         def affine(value):
             rows = value.shape[0]
@@ -190,6 +230,8 @@
             return jnp.dot(left, right, preferred_element_type=F32)
 
         clear()
+        for layer in range(wa.shape[0]):
+            prepare_a(layer)
 
         lane_in = lax.broadcasted_iota(jnp.int32, (LANES, LANES), 0)
         lane_out = lax.broadcasted_iota(jnp.int32, (LANES, LANES), 1)
@@ -197,44 +239,43 @@
         perm = jnp.where(lane_in == source, 1.0, 0.0).astype(BF16)
 
         def split_rows(first, second, pair, row):
-            one, two = mm(first, perm), mm(second, perm)
-            put_planes(pair, row, jnp.concatenate([one[:, :128], two[:, :128]], axis=1),
-                       jnp.concatenate([one[:, 128:], two[:, 128:]], axis=1))
+            put_planes(pair, row, jnp.concatenate([first[:, :128], second[:, :128]], axis=1),
+                       jnp.concatenate([first[:, 128:], second[:, 128:]], axis=1))
 
         def conv_a(layer, pair, row, rows):
             window = hs[pair, row:row + rows + 2].reshape((rows + 2) * 128, LANES)
             value = mm(wa[layer, 0:64 * rows, 0:128 * (rows + 2)], window)
-            tally(value)
             za[pl.ds(pair * ROWS_A + row, rows)] = value.reshape(rows, 64, LANES)
+            return value
 
         def norm_a(pair, row):
             value = norm_relu(za[pair * ROWS_A + row])
             put_planes(pair, row + 1, value[0:32], value[32:64])
 
-        @pl.loop(0, pairs)
+        @sweep
         def _(pair):
             x_copy(pair).wait()
+            both = mm(xv[pair].reshape(2 * ROWS_A * 32, LANES), perm).reshape(2, ROWS_A, 32, LANES)
             for row in range(ROWS_A):
-                split_rows(xv[pair, 0, row], xv[pair, 1, row], pair, row + 1)
-            for row in range(1, ROWS_A - 1, 2):
-                conv_a(0, pair, row, 2)
+                split_rows(both[0, row], both[1, row], pair, row + 1)
+            return tally(32, *[conv_a(0, pair, row, 2) for row in range(1, ROWS_A - 1, 2)])
 
         for side in range(2):
             settle(0, side, x_src[side], x_dst[side])
 
-        @pl.loop(0, pairs)
-        def _(pair):
-            split_rows(xh[0, 2 * pair], xh[0, 2 * pair + 1], pair, 0)
-            split_rows(xh[1, 2 * pair], xh[1, 2 * pair + 1], pair, ROWS_A + 1)
-            conv_a(0, pair, 0, 1)
-            conv_a(0, pair, ROWS_A - 1, 1)
-
-        moments(0, 32, count_a)
+        @sweep
+        def _(pair):
+            both = mm(xh[:, pl.ds(2 * pair, 2)].reshape(4 * 32, LANES), perm).reshape(2, 2, 32, LANES)
+            split_rows(both[0, 0], both[0, 1], pair, 0)
+            split_rows(both[1, 0], both[1, 1], pair, ROWS_A + 1)
+            return tally(32, conv_a(0, pair, 0, 1), conv_a(0, pair, ROWS_A - 1, 1))
+
+        moments(0, bn_a[0], count_a, prepare_down)
 
         a_src = (hs.at[:, ROWS_A, 32:96], hs.at[:, 1, 32:96])
         a_dst = (hs.at[:, 0, 32:96], hs.at[:, ROWS_A + 1, 32:96])
 
-        @pl.loop(0, pairs)
+        @sweep
         def _(pair):
             norm_a(pair, 0)
             norm_a(pair, ROWS_A - 1)
@@ -242,63 +283,60 @@
         for side in range(2):
             exchange(1, side, a_src[side], a_dst[side])
 
-        @pl.loop(0, pairs)
+        @sweep
         def _(pair):
             for row in range(1, ROWS_A - 1):
                 norm_a(pair, row)
-            for row in range(1, ROWS_A - 1, 2):
-                conv_a(1, pair, row, 2)
+            return tally(32, *[conv_a(1, pair, row, 2) for row in range(1, ROWS_A - 1, 2)])
 
         for side in range(2):
             settle(1, side, a_src[side], a_dst[side])
 
-        @pl.loop(0, pairs)
+        @sweep
         def _(pair):
             rebuild_a(pair, 0)
             rebuild_a(pair, ROWS_A + 1)
-            conv_a(1, pair, 0, 1)
-            conv_a(1, pair, ROWS_A - 1, 1)
-
-        moments(1, 32, count_a)
+            return tally(32, conv_a(1, pair, 0, 1), conv_a(1, pair, ROWS_A - 1, 1))
+
+        moments(1, bn_a[1], count_a, lambda: prepare_block(0))
 
         def conv_down(pair, row):
             window = hs[pair, 2 * row + 1:2 * row + 4].reshape(384, LANES)
             value = mm(wd[...], window)
-            tally(value)
             zb[pair * ROWS_B + row] = value
-
-        @pl.loop(0, pairs)
+            return value
+
+        @sweep
         def _(pair):
             norm_a(pair, 0)
 
         exchange(2, 1, a_src[1], a_dst[1])
 
-        @pl.loop(0, pairs)
+        @sweep
         def _(pair):
             for row in range(1, ROWS_A):
                 norm_a(pair, row)
-            for row in range(ROWS_B - 1):
-                conv_down(pair, row)
+            return tally(128, *[conv_down(pair, row) for row in range(ROWS_B - 1)])
 
         settle(2, 1, a_src[1], a_dst[1])
 
-        @pl.loop(0, pairs)
+        @sweep
         def _(pair):
             rebuild_a(pair, ROWS_A + 1)
-            conv_down(pair, ROWS_B - 1)
-
-        moments(2, 128, count_b)
+            return tally(128, conv_down(pair, ROWS_B - 1))
+
+        moments(2, bn_d[...], count_b, lambda: prepare_block(1))
 
         def conv_in(block, index, hidden):
             value = mm(wi[block], hidden)
-            tally(value)
             za[index] = value
+            return value
 
         def conv_mid(block, pair, row, rows):
             window = us[pair, row:row + rows + 2].reshape((rows + 2) * 192, LANES)
             value = mm(wm[block, 0:64 * rows, 0:192 * (rows + 2)], window)
-            tally(value)
             za[pl.ds(pair * ROWS_B + row, rows)] = value.reshape(rows, 64, LANES)
+            return value
 
         def norm_mid(pair, row):
             put_mid(pair, row + 1, norm_relu(za[pair * ROWS_B + row]))
@@ -306,20 +344,22 @@
         m_src = (us.at[:, ROWS_B, 64:128], us.at[:, 1, 64:128])
         m_dst = (us.at[:, 0, 64:128], us.at[:, ROWS_B + 1, 64:128])
 
-        @pl.loop(0, pairs)
-        def _(pair):
+        @sweep
+        def _(pair):
+            values = []
             for row in range(ROWS_B):
                 index = pair * ROWS_B + row
                 hidden = norm_relu(zb[index]).astype(BF16)
                 hb[index] = hidden
-                conv_in(0, index, hidden)
+                values.append(conv_in(0, index, hidden))
+            return tally(64, *values)
 
         blocks = wi.shape[0]
         for block in range(blocks):
             layer, step = 3 + 3 * block, 3 + block
-            moments(layer, 64, count_b)
-
-            @pl.loop(0, pairs)
+            moments(layer, bn_i[block], count_b, (lambda: prepare_block(2)) if block == 0 else None)
+
+            @sweep
             def _(pair):
                 norm_mid(pair, 0)
                 norm_mid(pair, ROWS_B - 1)
@@ -327,50 +367,52 @@
             for side in range(2):
                 exchange(step, side, m_src[side], m_dst[side])
 
-            @pl.loop(0, pairs)
+            @sweep
             def _(pair):
                 for row in range(1, ROWS_B - 1):
                     norm_mid(pair, row)
-                conv_mid(block, pair, 1, 2)
+                return tally(64, conv_mid(block, pair, 1, 2))
 
             for side in range(2):
                 settle(step, side, m_src[side], m_dst[side])
 
-            @pl.loop(0, pairs)
+            @sweep
             def _(pair):
                 rebuild_mid(pair, 0)
                 rebuild_mid(pair, ROWS_B + 1)
-                conv_mid(block, pair, 0, 1)
-                conv_mid(block, pair, ROWS_B - 1, 1)
-
-            moments(layer + 1, 64, count_b)
-
-            @pl.loop(0, pairs)
-            def _(pair):
+                return tally(64, conv_mid(block, pair, 0, 1), conv_mid(block, pair, ROWS_B - 1, 1))
+
+            moments(layer + 1, bn_m[block], count_b)
+
+            @sweep
+            def _(pair):
+                values = []
                 for row in range(ROWS_B):
                     index = pair * ROWS_B + row
-                    value = mm(wo[block], norm_relu(za[index]).astype(BF16))
-                    tally(value)
-                    zb[index] = value
-
-            moments(layer + 2, 128, count_b)
+                    values.append(mm(wo[block], norm_relu(za[index]).astype(BF16)))
+                    zb[index] = values[-1]
+                return tally(128, *values)
+
+            moments(layer + 2, bn_o[block], count_b)
 
             def finish(index):
                 return jnp.maximum(affine(zb[index]) + hb[index].astype(F32), 0.0)
 
             if block < blocks - 1:
-                @pl.loop(0, pairs)
+                @sweep
                 def _(pair):
+                    values = []
                     for row in range(ROWS_B):
                         index = pair * ROWS_B + row
                         hidden = finish(index).astype(BF16)
                         hb[index] = hidden
-                        conv_in(block + 1, index, hidden)
+                        values.append(conv_in(block + 1, index, hidden))
+                    return tally(64, *values)
             else:
                 def out_copy(pair):
                     return pltpu.make_async_copy(ov.at[pair], out_hbm.at[pl.ds(2 * pair, 2)], out_sem.at[pair])
 
-                @pl.loop(0, pairs)
+                @sweep
                 def _(pair):
                     for row in range(ROWS_B):
                         value = finish(pair * ROWS_B + row)
@@ -378,7 +420,7 @@
                             ov[pair, image, row] = value[:, image * 128:(image + 1) * 128].T.astype(BF16)
                     out_copy(pair).start()
 
-                @pl.loop(0, pairs)
+                @sweep
                 def _(pair):
                     out_copy(pair).wait()
 
@@ -386,16 +428,7 @@
         images_count = images.shape[0]
         pairs = images_count // 2
         x = jnp.transpose(images, (0, 1, 3, 2))
-        wa = jnp.stack([band(w_a[layer], 4, 4, (0, 1)) for layer in range(w_a.shape[0])])
-        wd = band(w_down, 3, 4, (1,))
-        wi = jnp.transpose(w_in, (0, 2, 1))
-        wm = jnp.stack([band(w_mid[block], 4, 3, (0,)) for block in range(w_mid.shape[0])])
-        wo = jnp.transpose(w_out, (0, 2, 1))
-        bn = [jnp.tile(bn_a[layer], (1, 4)) for layer in range(w_a.shape[0])] + [bn_down]
-        for block in range(w_in.shape[0]):
-            bn += [jnp.tile(bn_in[block], (1, 2)), jnp.tile(bn_mid[block], (1, 2)), bn_out[block]]
-        bn = jnp.stack(bn)
-        layers = bn.shape[0]
+        layers = w_a.shape[0] + 1 + 3 * w_in.shape[0]
         steps = 3 + w_in.shape[0]
         vmem = pl.BlockSpec(memory_space=pltpu.VMEM)
         hbm = pl.BlockSpec(memory_space=pl.ANY)
@@ -403,9 +436,13 @@
         return pl.pallas_call(
             kernel,
             out_shape=jax.ShapeDtypeStruct((images_count, ROWS_B, 128, 128), BF16),
-            in_specs=[hbm] + [vmem] * 6,
+            in_specs=[hbm] + [vmem] * 10,
             out_specs=hbm,
             scratch_shapes=[
+                pltpu.VMEM((w_a.shape[0], 128, 512), BF16),
+                pltpu.VMEM((128, 384), BF16),
+                pltpu.VMEM((w_in.shape[0], 128, 768), BF16),
+                pltpu.VMEM((w_in.shape[0], 128, 64), BF16),
                 pltpu.VMEM((pairs, 2, ROWS_A, 32, LANES), BF16),
                 pltpu.VMEM((2, images_count, 32, LANES), BF16),
                 pltpu.VMEM((pairs, ROWS_A + 2, 128, LANES), BF16),
@@ -423,7 +460,7 @@
             compiler_params=pltpu.CompilerParams(
                 collective_id=0, has_side_effects=True, vmem_limit_bytes=67043328),
             name="conv_stack",
-        )(x, wa, wd, wi, wm, wo, bn)
+        )(x, w_a, bn_a, w_down, bn_down, jnp.transpose(w_in, (0, 2, 1)), bn_in, w_mid, bn_mid, w_out, bn_out)
 
     act_spec = P("dp", "sp", None, None)
     return jax.shard_map(forward, mesh=mesh, in_specs=(act_spec,) + (P(),) * 10, out_specs=act_spec, check_vma=False)

time: 179 us -> 128 us (0.72)
  Pallas kernels: 153 us -> 123 us
  local copies, waits for them, and re-layouts: 23 us -> 4.79 us
  other arithmetic: 2.18 us -> 0 us
    pallas_call x1, Pallas kernels: 153 us -> 123 us  [forward(): pl.pallas_call(kernel, out_shape=jax.ShapeDtypeStruct((images_count, ROWS...]
    unnamed x13 -> x1, local copies, waits for them, and re-layouts: 14.6 us -> 4.79 us
    another operation x25 -> x0, local copies, waits for them, and re-layouts: 4.75 us -> none  [the longest x1 1.27 us: forward(): bn = jnp.stack(bn)]
    transpose x2 -> x0, local copies, waits for them, and re-layouts: 2.01 us -> none  [band(): kernel = jnp.transpose(weight, (3, 0, 1, 2))]
where the time goes in v2:
time: 128 us
  Pallas kernels  123 us (96%)
  local copies, waits for them, and re-layouts  4.79 us (4%)
    pallas_call x1, Pallas kernels, forward(): pl.pallas_call(kernel, out_shape=jax.ShapeDtypeStruct((images_count, ROWS...  123 us
    unnamed x1, local copies, waits for them, and re-layouts  4.79 us

profile of v2, /device:TPU:0, one launch (start us, length us, event | category | flops | bytes accessed | tf_op | source)
XLA Modules:
  0.0 128.1 jit_solution(5931604640526736145)
XLA Ops:
  0.0 123.3 %conv_stack.1 = bf16[32,4,128,128]{3,2,1,0:T(8,128)(2,1)} custom-call(bf16[32,8,32,256]{3,2,1,0:T(8,128)(2,1)} %bitcast.2, bf16[2,3,3,32,32]{4,3,2,1,0:T(8,128)(2,1)} %raw_a.1, f32[2,2,32]{2,1,0:T(2,128)} %bn_a.1, bf16[3,3,32,128]{3,2,1,0:T(8,128)(2,1)} %raw_d.1, f32[2,128]{1,0:T(2,128)} %bn_d.1, bf16[3,64,128]{2,1,0:T(8,128)(2,1)} %bitcast.3, ...), custom_call_target="tpu_custom_call" | custom-call | tf_op jit(solution)/shard_map/conv_stack/pallas_call | solution.py:436
  123.3 4.8 %copy.13 = bf16[32,4,128,128]{3,2,1,0:T(8,128)(2,1)} copy(bf16[32,4,128,128]{3,2,1,0:T(8,128)(2,1)} %conv_stack.1) | data formatting | bytes 8388608

commit v3 on v2

--- a/solution.py
+++ b/solution.py
@@ -1,3 +1,5 @@
+import functools
+
 import jax
 import jax.numpy as jnp
 from jax import lax
@@ -19,17 +21,21 @@
     groups = mesh.shape["sp"]
 
     def kernel(x_hbm, raw_a, bn_a, raw_d, bn_d, wi, bn_i, raw_m, bn_m, raw_o, bn_o, out_hbm,
-               wa, wd, wm, wo, xv, xh, hs, us, za, zb, hb, ov, acc, ab, stat,
+               perm, wa, wd, wm, wo, xv, xh, hs, us, za, zb, hb, ov, acc, ab, stat,
                x_sem, out_sem, halo_send, halo_recv, stat_send, stat_recv):
         pairs = xv.shape[0]
         me = lax.axis_index("sp")
         count_a = float(2 * pairs * ROWS_A * LANES * groups)
         count_b = float(2 * pairs * ROWS_B * 128 * groups)
 
-        def sweep(body, unroll=UNROLL):
-            @pl.loop(0, pairs // unroll)
+        def sweep(body, before=None, after=None):
+            @pl.loop(0, pairs // UNROLL)
             def _(step):
-                sums = [body(step * unroll + part) for part in range(unroll)]
+                if before is not None:
+                    before(step)
+                sums = [body(step * UNROLL + part) for part in range(UNROLL)]
+                if after is not None:
+                    after(step)
                 if sums[0] is not None:
                     channels = sums[0].shape[1]
                     acc[:, 0:channels] += sum(sums[1:], sums[0])
@@ -46,38 +52,44 @@
             pl.semaphore_signal(barrier, inc=1, device_id={"sp": lax.rem(me + hop, groups)}, device_id_type=MESH)
         pl.semaphore_wait(barrier, groups - 1)
 
-        def halo_copy(step, side, src, dst):
-            peer = me + 1 if side == 0 else me - 1
+        def halo_copy(step, side, chunk, refs, peer):
+            src, dst = refs[side](chunk * UNROLL)
             return pltpu.make_async_remote_copy(
-                src_ref=src, dst_ref=dst, send_sem=halo_send.at[step, side], recv_sem=halo_recv.at[step, side],
-                device_id={"sp": peer}, device_id_type=MESH)
-
-        def has_peer(side):
-            return me < groups - 1 if side == 0 else me > 0
-
-        def from_peer(side):
-            return me > 0 if side == 0 else me < groups - 1
-
-        def exchange(step, side, src, dst):
-            @pl.when(has_peer(side))
-            def _():
-                halo_copy(step, side, src, dst).start()
-
-        def settle(step, side, src, dst):
-            @pl.when(from_peer(side))
-            def _():
-                pltpu.make_async_remote_copy(
-                    src_ref=src, dst_ref=dst, send_sem=halo_send.at[step, side], recv_sem=halo_recv.at[step, side],
-                    device_id={"sp": me}, device_id_type=MESH).wait_recv()
-
-            @pl.when(has_peer(side))
-            def _():
-                halo_copy(step, side, src, dst).wait_send()
-
-        x_src = (x_hbm.at[:, ROWS_A - 1], x_hbm.at[:, 0])
-        x_dst = (xh.at[0], xh.at[1])
-        for side in range(2):
-            exchange(0, side, x_src[side], x_dst[side])
+                src_ref=src, dst_ref=dst, send_sem=halo_send.at[step, side, chunk],
+                recv_sem=halo_recv.at[step, side, chunk], device_id={"sp": peer}, device_id_type=MESH)
+
+        def exchange(step, refs, chunk, sides=(0, 1)):
+            for side in sides:
+                @pl.when(me < groups - 1 if side == 0 else me > 0)
+                def _():
+                    halo_copy(step, side, chunk, refs, me + 1 if side == 0 else me - 1).start()
+
+        def settle(step, refs, chunk, sides=(0, 1)):
+            for side in sides:
+                @pl.when(me > 0 if side == 0 else me < groups - 1)
+                def _():
+                    halo_copy(step, side, chunk, refs, me - 1 if side == 0 else me + 1).wait_recv()
+
+                @pl.when(me < groups - 1 if side == 0 else me > 0)
+                def _():
+                    halo_copy(step, side, chunk, refs, me + 1 if side == 0 else me - 1).wait_send()
+
+        def x_part(row, slot):
+            return lambda pair: (x_hbm.at[pl.ds(2 * pair, 2 * UNROLL), row], xh.at[slot, pl.ds(2 * pair, 2 * UNROLL)])
+
+        def h_part(row, slot):
+            return lambda pair: (hs.at[pl.ds(pair, UNROLL), row, 32:96], hs.at[pl.ds(pair, UNROLL), slot, 32:96])
+
+        def u_part(row, slot):
+            return lambda pair: (us.at[pl.ds(pair, UNROLL), row, 64:128], us.at[pl.ds(pair, UNROLL), slot, 64:128])
+
+        x_refs = (x_part(ROWS_A - 1, 0), x_part(0, 1))
+        h_refs = (h_part(ROWS_A, 0), h_part(1, ROWS_A + 1))
+        u_refs = (u_part(ROWS_B, 0), u_part(1, ROWS_B + 1))
+
+        @pl.loop(0, pairs // UNROLL)
+        def _(chunk):
+            exchange(0, x_refs, chunk)
 
         @pl.when(me == 0)
         def _():
@@ -176,7 +188,7 @@
         def moments(layer, params, count, during=None):
             channels = params.shape[1]
             for part in range(2):
-                turned = acc[part].T.reshape(16, 8, 128)
+                turned = jnp.concatenate([acc[part, 0:channels]] * (128 // channels), axis=0).T.reshape(16, 8, 128)
                 stat[layer, me, 8 * part:8 * part + 8] = jnp.sum(turned, axis=0)
             copies = []
             for hop in range(1, groups):
@@ -202,20 +214,15 @@
                 total = total + stat[layer, origin]
 
             def fold(block):
-                line = jnp.broadcast_to(jnp.sum(block, axis=0, keepdims=True), (8, 128))
-                width = 64
-                while width >= channels:
-                    line = line + pltpu.roll(line, width, 1)
-                    width //= 2
-                return line / count
+                return jnp.sum(block, axis=0, keepdims=True) / count
 
             mean, square = fold(total[0:8]), fold(total[8:16])
             var = square - mean * mean
             wide = jnp.concatenate([params] * (128 // channels), axis=1)
             scale = wide[0:1] * lax.rsqrt(var + NORM_EPS)
             bias = wide[1:2] - mean * scale
-            ab[0] = jnp.broadcast_to(scale[0:1], (128, 128)).T
-            ab[1] = jnp.broadcast_to(bias[0:1], (128, 128)).T
+            ab[0] = jnp.broadcast_to(scale, (128, 128)).T
+            ab[1] = jnp.broadcast_to(bias, (128, 128)).T
 
         def affine(value):
             rows = value.shape[0]
@@ -236,7 +243,7 @@
         lane_in = lax.broadcasted_iota(jnp.int32, (LANES, LANES), 0)
         lane_out = lax.broadcasted_iota(jnp.int32, (LANES, LANES), 1)
         source = jnp.where(lane_out < 128, 2 * lane_out, 2 * lane_out - (LANES - 1))
-        perm = jnp.where(lane_in == source, 1.0, 0.0).astype(BF16)
+        perm[...] = jnp.where(lane_in == source, 1.0, 0.0).astype(BF16)
 
         def split_rows(first, second, pair, row):
             put_planes(pair, row, jnp.concatenate([first[:, :128], second[:, :128]], axis=1),
@@ -255,33 +262,24 @@
         @sweep
         def _(pair):
             x_copy(pair).wait()
-            both = mm(xv[pair].reshape(2 * ROWS_A * 32, LANES), perm).reshape(2, ROWS_A, 32, LANES)
+            both = mm(xv[pair].reshape(2 * ROWS_A * 32, LANES), perm[...]).reshape(2, ROWS_A, 32, LANES)
             for row in range(ROWS_A):
                 split_rows(both[0, row], both[1, row], pair, row + 1)
             return tally(32, *[conv_a(0, pair, row, 2) for row in range(1, ROWS_A - 1, 2)])
 
-        for side in range(2):
-            settle(0, side, x_src[side], x_dst[side])
-
-        @sweep
-        def _(pair):
-            both = mm(xh[:, pl.ds(2 * pair, 2)].reshape(4 * 32, LANES), perm).reshape(2, 2, 32, LANES)
+        @functools.partial(sweep, before=lambda chunk: settle(0, x_refs, chunk))
+        def _(pair):
+            both = mm(xh[:, pl.ds(2 * pair, 2)].reshape(4 * 32, LANES), perm[...]).reshape(2, 2, 32, LANES)
             split_rows(both[0, 0], both[0, 1], pair, 0)
             split_rows(both[1, 0], both[1, 1], pair, ROWS_A + 1)
             return tally(32, conv_a(0, pair, 0, 1), conv_a(0, pair, ROWS_A - 1, 1))
 
         moments(0, bn_a[0], count_a, prepare_down)
 
-        a_src = (hs.at[:, ROWS_A, 32:96], hs.at[:, 1, 32:96])
-        a_dst = (hs.at[:, 0, 32:96], hs.at[:, ROWS_A + 1, 32:96])
-
-        @sweep
+        @functools.partial(sweep, after=lambda chunk: exchange(1, h_refs, chunk))
         def _(pair):
             norm_a(pair, 0)
             norm_a(pair, ROWS_A - 1)
-
-        for side in range(2):
-            exchange(1, side, a_src[side], a_dst[side])
 
         @sweep
         def _(pair):
@@ -289,10 +287,7 @@
                 norm_a(pair, row)
             return tally(32, *[conv_a(1, pair, row, 2) for row in range(1, ROWS_A - 1, 2)])
 
-        for side in range(2):
-            settle(1, side, a_src[side], a_dst[side])
-
-        @sweep
+        @functools.partial(sweep, before=lambda chunk: settle(1, h_refs, chunk))
         def _(pair):
             rebuild_a(pair, 0)
             rebuild_a(pair, ROWS_A + 1)
@@ -306,11 +301,9 @@
             zb[pair * ROWS_B + row] = value
             return value
 
-        @sweep
+        @functools.partial(sweep, after=lambda chunk: exchange(2, h_refs, chunk, (1,)))
         def _(pair):
             norm_a(pair, 0)
-
-        exchange(2, 1, a_src[1], a_dst[1])
 
         @sweep
         def _(pair):
@@ -318,9 +311,7 @@
                 norm_a(pair, row)
             return tally(128, *[conv_down(pair, row) for row in range(ROWS_B - 1)])
 
-        settle(2, 1, a_src[1], a_dst[1])
-
-        @sweep
+        @functools.partial(sweep, before=lambda chunk: settle(2, h_refs, chunk, (1,)))
         def _(pair):
             rebuild_a(pair, ROWS_A + 1)
             return tally(128, conv_down(pair, ROWS_B - 1))
@@ -340,9 +331,6 @@
 
         def norm_mid(pair, row):
             put_mid(pair, row + 1, norm_relu(za[pair * ROWS_B + row]))
-
-        m_src = (us.at[:, ROWS_B, 64:128], us.at[:, 1, 64:128])
-        m_dst = (us.at[:, 0, 64:128], us.at[:, ROWS_B + 1, 64:128])
 
         @sweep
         def _(pair):
@@ -359,13 +347,10 @@
             layer, step = 3 + 3 * block, 3 + block
             moments(layer, bn_i[block], count_b, (lambda: prepare_block(2)) if block == 0 else None)
 
-            @sweep
+            @functools.partial(sweep, after=lambda chunk: exchange(step, u_refs, chunk))
             def _(pair):
                 norm_mid(pair, 0)
                 norm_mid(pair, ROWS_B - 1)
-
-            for side in range(2):
-                exchange(step, side, m_src[side], m_dst[side])
 
             @sweep
             def _(pair):
@@ -373,10 +358,7 @@
                     norm_mid(pair, row)
                 return tally(64, conv_mid(block, pair, 1, 2))
 
-            for side in range(2):
-                settle(step, side, m_src[side], m_dst[side])
-
-            @sweep
+            @functools.partial(sweep, before=lambda chunk: settle(step, u_refs, chunk))
             def _(pair):
                 rebuild_mid(pair, 0)
                 rebuild_mid(pair, ROWS_B + 1)
@@ -439,6 +421,7 @@
             in_specs=[hbm] + [vmem] * 10,
             out_specs=hbm,
             scratch_shapes=[
+                pltpu.VMEM((LANES, LANES), BF16),
                 pltpu.VMEM((w_a.shape[0], 128, 512), BF16),
                 pltpu.VMEM((128, 384), BF16),
                 pltpu.VMEM((w_in.shape[0], 128, 768), BF16),
@@ -454,7 +437,7 @@
                 pltpu.VMEM((2, 128, 128), F32),
                 pltpu.VMEM((2, 128, 128), F32),
                 pltpu.VMEM((layers, groups, 16, 128), F32),
-                dma((pairs,)), dma((pairs,)), dma((steps, 2)), dma((steps, 2)),
+                dma((pairs,)), dma((pairs,)), dma((steps, 2, pairs // UNROLL)), dma((steps, 2, pairs // UNROLL)),
                 dma((layers, groups)), dma((layers, groups)),
             ],
             compiler_params=pltpu.CompilerParams(

time: 128 us -> 118 us (0.922)
  Pallas kernels: 123 us -> 113 us
    pallas_call x1, Pallas kernels: 123 us -> 113 us  [forward(): pl.pallas_call(kernel, out_shape=jax.ShapeDtypeStruct((images_count, ROWS...]
where the time goes in v3:
time: 118 us; the launch traced here: 117 us
  Pallas kernels  113 us (96%)
  local copies, waits for them, and re-layouts  4.79 us (4%)
    pallas_call x1, Pallas kernels, forward(): pl.pallas_call(kernel, out_shape=jax.ShapeDtypeStruct((images_count, ROWS...  113 us
    unnamed x1, local copies, waits for them, and re-layouts  4.79 us

profile of v3, /device:TPU:0, one launch (start us, length us, event | category | flops | bytes accessed | tf_op | source)
XLA Modules:
  0.0 117.4 jit_solution(14197047517642791978)
XLA Ops:
  0.0 112.7 %conv_stack.1 = bf16[32,4,128,128]{3,2,1,0:T(8,128)(2,1)} custom-call(bf16[32,8,32,256]{3,2,1,0:T(8,128)(2,1)} %bitcast.2, bf16[2,3,3,32,32]{4,3,2,1,0:T(8,128)(2,1)} %raw_a.1, f32[2,2,32]{2,1,0:T(2,128)} %bn_a.1, bf16[3,3,32,128]{3,2,1,0:T(8,128)(2,1)} %raw_d.1, f32[2,128]{1,0:T(2,128)} %bn_d.1, bf16[3,64,128]{2,1,0:T(8,128)(2,1)} %bitcast.3, ...), custom_call_target="tpu_custom_call" | custom-call | tf_op jit(solution)/shard_map/conv_stack/pallas_call | solution.py:418
  112.7 4.8 %copy.13 = bf16[32,4,128,128]{3,2,1,0:T(8,128)(2,1)} copy(bf16[32,4,128,128]{3,2,1,0:T(8,128)(2,1)} %conv_stack.1) | data formatting | bytes 8388608

commit v4 on v3

--- a/solution.py
+++ b/solution.py
@@ -20,7 +20,8 @@
 def solution(mesh):
     groups = mesh.shape["sp"]
 
-    def kernel(x_hbm, raw_a, bn_a, raw_d, bn_d, wi, bn_i, raw_m, bn_m, raw_o, bn_o, out_hbm,
+    def kernel(x_hbm, raw_a_hbm, bn_a, raw_d_hbm, bn_d, wi_hbm, bn_i, raw_m_hbm, bn_m, raw_o_hbm, bn_o, out_hbm,
+               raw_a, raw_d, wi, raw_m, raw_o, w_sem,
                perm, wa, wd, wm, wo, xv, xh, hs, us, za, zb, hb, ov, acc, ab, stat,
                x_sem, out_sem, halo_send, halo_recv, stat_send, stat_recv):
         pairs = xv.shape[0]
@@ -28,12 +29,13 @@
         count_a = float(2 * pairs * ROWS_A * LANES * groups)
         count_b = float(2 * pairs * ROWS_B * 128 * groups)
 
-        def sweep(body, before=None, after=None):
+        def sweep(body, *later, before=None, after=None):
             @pl.loop(0, pairs // UNROLL)
             def _(step):
                 if before is not None:
                     before(step)
-                sums = [body(step * UNROLL + part) for part in range(UNROLL)]
+                for stage in (body,) + later:
+                    sums = [stage(step * UNROLL + part) for part in range(UNROLL)]
                 if after is not None:
                     after(step)
                 if sums[0] is not None:
@@ -46,6 +48,11 @@
         @sweep
         def _(pair):
             x_copy(pair).start()
+
+        loads = [pltpu.make_async_copy(src, dst, w_sem.at[index]) for index, (src, dst) in enumerate(
+            [(raw_a_hbm, raw_a), (raw_d_hbm, raw_d), (raw_m_hbm, raw_m), (raw_o_hbm, raw_o), (wi_hbm, wi)])]
+        for load in loads:
+            load.start()
 
         barrier = pltpu.get_barrier_semaphore()
         for hop in range(1, groups):
@@ -237,8 +244,8 @@
             return jnp.dot(left, right, preferred_element_type=F32)
 
         clear()
-        for layer in range(wa.shape[0]):
-            prepare_a(layer)
+        loads[0].wait()
+        prepare_a(0)
 
         lane_in = lax.broadcasted_iota(jnp.int32, (LANES, LANES), 0)
         lane_out = lax.broadcasted_iota(jnp.int32, (LANES, LANES), 1)
@@ -259,41 +266,52 @@
             value = norm_relu(za[pair * ROWS_A + row])
             put_planes(pair, row + 1, value[0:32], value[32:64])
 
-        @sweep
-        def _(pair):
+        def planes(pair):
             x_copy(pair).wait()
             both = mm(xv[pair].reshape(2 * ROWS_A * 32, LANES), perm[...]).reshape(2, ROWS_A, 32, LANES)
             for row in range(ROWS_A):
                 split_rows(both[0, row], both[1, row], pair, row + 1)
-            return tally(32, *[conv_a(0, pair, row, 2) for row in range(1, ROWS_A - 1, 2)])
-
-        @functools.partial(sweep, before=lambda chunk: settle(0, x_refs, chunk))
-        def _(pair):
+
+        def inner_a(layer):
+            return lambda pair: tally(32, *[conv_a(layer, pair, row, 2) for row in range(1, ROWS_A - 1, 2)])
+
+        def outer_a(layer):
+            return lambda pair: tally(32, conv_a(layer, pair, 0, 1), conv_a(layer, pair, ROWS_A - 1, 1))
+
+        sweep(planes, inner_a(0))
+
+        def halo_planes(pair):
             both = mm(xh[:, pl.ds(2 * pair, 2)].reshape(4 * 32, LANES), perm[...]).reshape(2, 2, 32, LANES)
             split_rows(both[0, 0], both[0, 1], pair, 0)
             split_rows(both[1, 0], both[1, 1], pair, ROWS_A + 1)
-            return tally(32, conv_a(0, pair, 0, 1), conv_a(0, pair, ROWS_A - 1, 1))
-
-        moments(0, bn_a[0], count_a, prepare_down)
+
+        sweep(halo_planes, outer_a(0), before=lambda chunk: settle(0, x_refs, chunk))
+
+        def second_weights():
+            for load in loads[1:]:
+                load.wait()
+            prepare_a(1)
+
+        moments(0, bn_a[0], count_a, second_weights)
 
         @functools.partial(sweep, after=lambda chunk: exchange(1, h_refs, chunk))
         def _(pair):
             norm_a(pair, 0)
             norm_a(pair, ROWS_A - 1)
 
-        @sweep
-        def _(pair):
+        def norm_inner(pair):
             for row in range(1, ROWS_A - 1):
                 norm_a(pair, row)
-            return tally(32, *[conv_a(1, pair, row, 2) for row in range(1, ROWS_A - 1, 2)])
-
-        @functools.partial(sweep, before=lambda chunk: settle(1, h_refs, chunk))
-        def _(pair):
+
+        sweep(norm_inner, inner_a(1))
+
+        def rebuild_both(pair):
             rebuild_a(pair, 0)
             rebuild_a(pair, ROWS_A + 1)
-            return tally(32, conv_a(1, pair, 0, 1), conv_a(1, pair, ROWS_A - 1, 1))
-
-        moments(1, bn_a[1], count_a, lambda: prepare_block(0))
+
+        sweep(rebuild_both, outer_a(1), before=lambda chunk: settle(1, h_refs, chunk))
+
+        moments(1, bn_a[1], count_a, prepare_down)
 
         def conv_down(pair, row):
             window = hs[pair, 2 * row + 1:2 * row + 4].reshape(384, LANES)
@@ -305,21 +323,18 @@
         def _(pair):
             norm_a(pair, 0)
 
-        @sweep
-        def _(pair):
+        def norm_below(pair):
             for row in range(1, ROWS_A):
                 norm_a(pair, row)
-            return tally(128, *[conv_down(pair, row) for row in range(ROWS_B - 1)])
-
-        @functools.partial(sweep, before=lambda chunk: settle(2, h_refs, chunk, (1,)))
-        def _(pair):
-            rebuild_a(pair, ROWS_A + 1)
-            return tally(128, conv_down(pair, ROWS_B - 1))
-
-        moments(2, bn_d[...], count_b, lambda: prepare_block(1))
-
-        def conv_in(block, index, hidden):
-            value = mm(wi[block], hidden)
+
+        sweep(norm_below, lambda pair: tally(128, *[conv_down(pair, row) for row in range(ROWS_B - 1)]))
+        sweep(lambda pair: rebuild_a(pair, ROWS_A + 1), lambda pair: tally(128, conv_down(pair, ROWS_B - 1)),
+              before=lambda chunk: settle(2, h_refs, chunk, (1,)))
+
+        moments(2, bn_d[...], count_b, lambda: prepare_block(0))
+
+        def conv_in(block, index):
+            value = mm(wi[block], hb[index])
             za[index] = value
             return value
 
@@ -332,37 +347,38 @@
         def norm_mid(pair, row):
             put_mid(pair, row + 1, norm_relu(za[pair * ROWS_B + row]))
 
-        @sweep
-        def _(pair):
-            values = []
+        def all_in(block):
+            return lambda pair: tally(64, *[conv_in(block, pair * ROWS_B + row) for row in range(ROWS_B)])
+
+        def first_hidden(pair):
             for row in range(ROWS_B):
                 index = pair * ROWS_B + row
-                hidden = norm_relu(zb[index]).astype(BF16)
-                hb[index] = hidden
-                values.append(conv_in(0, index, hidden))
-            return tally(64, *values)
+                hb[index] = norm_relu(zb[index]).astype(BF16)
+
+        sweep(first_hidden, all_in(0))
 
         blocks = wi.shape[0]
         for block in range(blocks):
             layer, step = 3 + 3 * block, 3 + block
-            moments(layer, bn_i[block], count_b, (lambda: prepare_block(2)) if block == 0 else None)
+            moments(layer, bn_i[block], count_b, (lambda: prepare_block(block + 1)) if block < blocks - 1 else None)
 
             @functools.partial(sweep, after=lambda chunk: exchange(step, u_refs, chunk))
             def _(pair):
                 norm_mid(pair, 0)
                 norm_mid(pair, ROWS_B - 1)
 
-            @sweep
-            def _(pair):
+            def mid_inner(pair):
                 for row in range(1, ROWS_B - 1):
                     norm_mid(pair, row)
-                return tally(64, conv_mid(block, pair, 1, 2))
-
-            @functools.partial(sweep, before=lambda chunk: settle(step, u_refs, chunk))
-            def _(pair):
+
+            def mid_outer(pair):
                 rebuild_mid(pair, 0)
                 rebuild_mid(pair, ROWS_B + 1)
-                return tally(64, conv_mid(block, pair, 0, 1), conv_mid(block, pair, ROWS_B - 1, 1))
+
+            sweep(mid_inner, lambda pair: tally(64, conv_mid(block, pair, 1, 2)))
+            sweep(mid_outer,
+                  lambda pair: tally(64, conv_mid(block, pair, 0, 1), conv_mid(block, pair, ROWS_B - 1, 1)),
+                  before=lambda chunk: settle(step, u_refs, chunk))
 
             moments(layer + 1, bn_m[block], count_b)
 
@@ -381,15 +397,12 @@
                 return jnp.maximum(affine(zb[index]) + hb[index].astype(F32), 0.0)
 
             if block < blocks - 1:
-                @sweep
-                def _(pair):
-                    values = []
+                def next_hidden(pair):
                     for row in range(ROWS_B):
                         index = pair * ROWS_B + row
-                        hidden = finish(index).astype(BF16)
-                        hb[index] = hidden
-                        values.append(conv_in(block + 1, index, hidden))
-                    return tally(64, *values)
+                        hb[index] = finish(index).astype(BF16)
+
+                sweep(next_hidden, all_in(block + 1))
             else:
                 def out_copy(pair):
                     return pltpu.make_async_copy(ov.at[pair], out_hbm.at[pl.ds(2 * pair, 2)], out_sem.at[pair])
@@ -418,9 +431,11 @@
         return pl.pallas_call(
             kernel,
             out_shape=jax.ShapeDtypeStruct((images_count, ROWS_B, 128, 128), BF16),
-            in_specs=[hbm] + [vmem] * 10,
+            in_specs=[hbm] + [hbm, vmem] * 5,
             out_specs=hbm,
             scratch_shapes=[
+                pltpu.VMEM(w_a.shape, BF16), pltpu.VMEM(w_down.shape, BF16), pltpu.VMEM((w_in.shape[0], 64, 128), BF16),
+                pltpu.VMEM(w_mid.shape, BF16), pltpu.VMEM(w_out.shape, BF16), dma((5,)),
                 pltpu.VMEM((LANES, LANES), BF16),
                 pltpu.VMEM((w_a.shape[0], 128, 512), BF16),
                 pltpu.VMEM((128, 384), BF16),

time: 118 us -> 113 us (0.958)
  Pallas kernels: 113 us -> 108 us
    pallas_call x1, Pallas kernels: 113 us -> 108 us  [forward(): pl.pallas_call(kernel, out_shape=jax.ShapeDtypeStruct((images_count, ROWS...]
where the time goes in v4:
time: 113 us
  Pallas kernels  108 us (96%)
  local copies, waits for them, and re-layouts  4.79 us (4%)
    pallas_call x1, Pallas kernels, forward(): pl.pallas_call(kernel, out_shape=jax.ShapeDtypeStruct((images_count, ROWS...  108 us
    unnamed x1, local copies, waits for them, and re-layouts  4.79 us

profile of v4, /device:TPU:0, one launch (start us, length us, event | category | flops | bytes accessed | tf_op | source)
XLA Modules:
  0.0 112.7 jit_solution(15165569561973341713)
XLA Ops:
  0.0 107.9 %conv_stack.1 = bf16[32,4,128,128]{3,2,1,0:T(8,128)(2,1)} custom-call(bf16[32,8,32,256]{3,2,1,0:T(8,128)(2,1)} %bitcast.2, bf16[2,3,3,32,32]{4,3,2,1,0:T(8,128)(2,1)} %raw_a_hbm.1, f32[2,2,32]{2,1,0:T(2,128)} %bn_a.1, bf16[3,3,32,128]{3,2,1,0:T(8,128)(2,1)} %raw_d_hbm.1, f32[2,128]{1,0:T(2,128)} %bn_d.1, bf16[3,64,128]{2,1,0:T(8,128)(2,1)} %bitcast.3, ...), custom_call_target="tpu_custom_call" | custom-call | tf_op jit(solution)/shard_map/conv_stack/pallas_call | solution.py:431
  107.9 4.8 %copy.13 = bf16[32,4,128,128]{3,2,1,0:T(8,128)(2,1)} copy(bf16[32,4,128,128]{3,2,1,0:T(8,128)(2,1)} %conv_stack.1) | data formatting | bytes 8388608

commit v5 on v4

--- a/solution.py
+++ b/solution.py
@@ -23,14 +23,14 @@
     def kernel(x_hbm, raw_a_hbm, bn_a, raw_d_hbm, bn_d, wi_hbm, bn_i, raw_m_hbm, bn_m, raw_o_hbm, bn_o, out_hbm,
                raw_a, raw_d, wi, raw_m, raw_o, w_sem,
                perm, wa, wd, wm, wo, xv, xh, hs, us, za, zb, hb, ov, acc, ab, stat,
-               x_sem, out_sem, halo_send, halo_recv, stat_send, stat_recv):
+               x_sem, out_sem, halo_send, halo_recv, zh, early_send, early_recv, stat_send, stat_recv):
         pairs = xv.shape[0]
         me = lax.axis_index("sp")
         count_a = float(2 * pairs * ROWS_A * LANES * groups)
         count_b = float(2 * pairs * ROWS_B * 128 * groups)
 
-        def sweep(body, *later, before=None, after=None):
-            @pl.loop(0, pairs // UNROLL)
+        def sweep(body, *later, before=None, after=None, first=0):
+            @pl.loop(first, pairs // UNROLL)
             def _(step):
                 if before is not None:
                     before(step)
@@ -89,6 +89,39 @@
 
         def u_part(row, slot):
             return lambda pair: (us.at[pl.ds(pair, UNROLL), row, 64:128], us.at[pl.ds(pair, UNROLL), slot, 64:128])
+
+        def early_copy(step, side, part, rows, peer):
+            return pltpu.make_async_remote_copy(
+                src_ref=za.at[part * rows + (rows - 1 if side == 0 else 0)], dst_ref=zh.at[step, side, part],
+                send_sem=early_send.at[step, side, part], recv_sem=early_recv.at[step, side, part],
+                device_id={"sp": peer}, device_id_type=MESH)
+
+        def early(step, rows, sides=(0, 1)):
+            for side in sides:
+                @pl.when(me < groups - 1 if side == 0 else me > 0)
+                def _():
+                    for part in range(UNROLL):
+                        early_copy(step, side, part, rows, me + 1 if side == 0 else me - 1).start()
+
+        def settle_early(step, rows, put, sides=(0, 1)):
+            for side in sides:
+                @pl.when(me > 0 if side == 0 else me < groups - 1)
+                def _():
+                    for part in range(UNROLL):
+                        early_copy(step, side, part, rows, me - 1 if side == 0 else me + 1).wait_recv()
+                    for part in range(UNROLL):
+                        put(part, 0 if side == 0 else rows + 1, norm_relu(zh[step, side, part]))
+
+                @pl.when(me < groups - 1 if side == 0 else me > 0)
+                def _():
+                    for part in range(UNROLL):
+                        early_copy(step, side, part, rows, me + 1 if side == 0 else me - 1).wait_send()
+
+        def first_chunk(*stages):
+            for stage in stages:
+                sums = [stage(part) for part in range(UNROLL)]
+            if sums[0] is not None:
+                acc[:, 0:sums[0].shape[1]] += sum(sums[1:], sums[0])
 
         x_refs = (x_part(ROWS_A - 1, 0), x_part(0, 1))
         h_refs = (h_part(ROWS_A, 0), h_part(1, ROWS_A + 1))
@@ -192,7 +225,7 @@
                         total, square = total + piece, square + piece * piece
             return jnp.stack([total, square])
 
-        def moments(layer, params, count, during=None):
+        def moments(layer, params, count, during=None, early=None):
             channels = params.shape[1]
             for part in range(2):
                 turned = jnp.concatenate([acc[part, 0:channels]] * (128 // channels), axis=0).T.reshape(16, 8, 128)
@@ -205,6 +238,8 @@
                     device_id={"sp": lax.rem(me + hop, groups)}, device_id_type=MESH))
             for copy in copies:
                 copy.start()
+            if early is not None:
+                early()
             clear()
             if during is not None:
                 during()
@@ -292,12 +327,17 @@
                 load.wait()
             prepare_a(1)
 
-        moments(0, bn_a[0], count_a, second_weights)
-
-        @functools.partial(sweep, after=lambda chunk: exchange(1, h_refs, chunk))
-        def _(pair):
+        moments(0, bn_a[0], count_a, second_weights, lambda: early(1, ROWS_A))
+
+        def norm_edges(pair):
             norm_a(pair, 0)
             norm_a(pair, ROWS_A - 1)
+
+        def put_edge(pair, slot, value):
+            put_planes(pair, slot, value[0:32], value[32:64])
+
+        sweep(norm_edges, after=lambda chunk: exchange(1, h_refs, chunk), first=1)
+        first_chunk(norm_edges)
 
         def norm_inner(pair):
             for row in range(1, ROWS_A - 1):
@@ -309,9 +349,11 @@
             rebuild_a(pair, 0)
             rebuild_a(pair, ROWS_A + 1)
 
-        sweep(rebuild_both, outer_a(1), before=lambda chunk: settle(1, h_refs, chunk))
-
-        moments(1, bn_a[1], count_a, prepare_down)
+        settle_early(1, ROWS_A, put_edge)
+        first_chunk(outer_a(1))
+        sweep(rebuild_both, outer_a(1), before=lambda chunk: settle(1, h_refs, chunk), first=1)
+
+        moments(1, bn_a[1], count_a, prepare_down, lambda: early(2, ROWS_A, (1,)))
 
         def conv_down(pair, row):
             window = hs[pair, 2 * row + 1:2 * row + 4].reshape(384, LANES)
@@ -319,17 +361,22 @@
             zb[pair * ROWS_B + row] = value
             return value
 
-        @functools.partial(sweep, after=lambda chunk: exchange(2, h_refs, chunk, (1,)))
-        def _(pair):
-            norm_a(pair, 0)
+        sweep(lambda pair: norm_a(pair, 0), after=lambda chunk: exchange(2, h_refs, chunk, (1,)), first=1)
+        first_chunk(lambda pair: norm_a(pair, 0))
 
         def norm_below(pair):
             for row in range(1, ROWS_A):
                 norm_a(pair, row)
 
         sweep(norm_below, lambda pair: tally(128, *[conv_down(pair, row) for row in range(ROWS_B - 1)]))
-        sweep(lambda pair: rebuild_a(pair, ROWS_A + 1), lambda pair: tally(128, conv_down(pair, ROWS_B - 1)),
-              before=lambda chunk: settle(2, h_refs, chunk, (1,)))
+
+        def down_edge(pair):
+            return tally(128, conv_down(pair, ROWS_B - 1))
+
+        settle_early(2, ROWS_A, put_edge, (1,))
+        first_chunk(down_edge)
+        sweep(lambda pair: rebuild_a(pair, ROWS_A + 1), down_edge,
+              before=lambda chunk: settle(2, h_refs, chunk, (1,)), first=1)
 
         moments(2, bn_d[...], count_b, lambda: prepare_block(0))
 
@@ -360,12 +407,18 @@
         blocks = wi.shape[0]
         for block in range(blocks):
             layer, step = 3 + 3 * block, 3 + block
-            moments(layer, bn_i[block], count_b, (lambda: prepare_block(block + 1)) if block < blocks - 1 else None)
-
-            @functools.partial(sweep, after=lambda chunk: exchange(step, u_refs, chunk))
-            def _(pair):
+            moments(layer, bn_i[block], count_b, (lambda: prepare_block(block + 1)) if block < blocks - 1 else None,
+                    lambda: early(step, ROWS_B))
+
+            def mid_edges(pair):
                 norm_mid(pair, 0)
                 norm_mid(pair, ROWS_B - 1)
+
+            def mid_conv(pair):
+                return tally(64, conv_mid(block, pair, 0, 1), conv_mid(block, pair, ROWS_B - 1, 1))
+
+            sweep(mid_edges, after=lambda chunk: exchange(step, u_refs, chunk), first=1)
+            first_chunk(mid_edges)
 
             def mid_inner(pair):
                 for row in range(1, ROWS_B - 1):
@@ -376,9 +429,9 @@
                 rebuild_mid(pair, ROWS_B + 1)
 
             sweep(mid_inner, lambda pair: tally(64, conv_mid(block, pair, 1, 2)))
-            sweep(mid_outer,
-                  lambda pair: tally(64, conv_mid(block, pair, 0, 1), conv_mid(block, pair, ROWS_B - 1, 1)),
-                  before=lambda chunk: settle(step, u_refs, chunk))
+            settle_early(step, ROWS_B, put_mid)
+            first_chunk(mid_conv)
+            sweep(mid_outer, mid_conv, before=lambda chunk: settle(step, u_refs, chunk), first=1)
 
             moments(layer + 1, bn_m[block], count_b)
 
@@ -453,6 +506,7 @@
                 pltpu.VMEM((2, 128, 128), F32),
                 pltpu.VMEM((layers, groups, 16, 128), F32),
                 dma((pairs,)), dma((pairs,)), dma((steps, 2, pairs // UNROLL)), dma((steps, 2, pairs // UNROLL)),
+                pltpu.VMEM((steps, 2, UNROLL, 64, LANES), F32), dma((steps, 2, UNROLL)), dma((steps, 2, UNROLL)),
                 dma((layers, groups)), dma((layers, groups)),
             ],
             compiler_params=pltpu.CompilerParams(

time: 113 us -> 109 us (0.965)
  Pallas kernels: 108 us -> 104 us
    pallas_call x1, Pallas kernels: 108 us -> 104 us  [forward(): pl.pallas_call(kernel, out_shape=jax.ShapeDtypeStruct((images_count, ROWS...]
where the time goes in v5:
time: 109 us; the launch traced here: 108 us
  Pallas kernels  104 us (95%)
  local copies, waits for them, and re-layouts  4.79 us (4%)
    pallas_call x1, Pallas kernels, forward(): pl.pallas_call(kernel, out_shape=jax.ShapeDtypeStruct((images_count, ROWS...  104 us
    unnamed x1, local copies, waits for them, and re-layouts  4.79 us

profile of v5, /device:TPU:0, one launch (start us, length us, event | category | flops | bytes accessed | tf_op | source)
XLA Modules:
  0.0 108.4 jit_solution(5208414616836022932)
XLA Ops:
  0.0 103.6 %conv_stack.1 = bf16[32,4,128,128]{3,2,1,0:T(8,128)(2,1)} custom-call(bf16[32,8,32,256]{3,2,1,0:T(8,128)(2,1)} %bitcast.2, bf16[2,3,3,32,32]{4,3,2,1,0:T(8,128)(2,1)} %raw_a_hbm.1, f32[2,2,32]{2,1,0:T(2,128)} %bn_a.1, bf16[3,3,32,128]{3,2,1,0:T(8,128)(2,1)} %raw_d_hbm.1, f32[2,128]{1,0:T(2,128)} %bn_d.1, bf16[3,64,128]{2,1,0:T(8,128)(2,1)} %bitcast.3, ...), custom_call_target="tpu_custom_call" | custom-call | tf_op jit(solution)/shard_map/conv_stack/pallas_call | solution.py:484
  103.6 4.8 %copy.13 = bf16[32,4,128,128]{3,2,1,0:T(8,128)(2,1)} copy(bf16[32,4,128,128]{3,2,1,0:T(8,128)(2,1)} %conv_stack.1) | data formatting | bytes 8388608

commit v6 on v5

--- a/solution.py
+++ b/solution.py
@@ -14,20 +14,33 @@
 ROWS_A = 8
 ROWS_B = 4
 UNROLL = 4
+LAST_STEPS = 4
 LANES = 256
+HALF = 128
+MID = 64
+CIN = 32
+THREE = 96
+TRIPLE = 192
+DOWN_K = 384
+BAND_A = 512
+BAND_B = 768
+FOUR = 4
+SUB = 8
+PAIR_SUB = 16
 
 
 def solution(mesh):
     groups = mesh.shape["sp"]
 
-    def kernel(x_hbm, raw_a_hbm, bn_a, raw_d_hbm, bn_d, wi_hbm, bn_i, raw_m_hbm, bn_m, raw_o_hbm, bn_o, out_hbm,
+    def kernel(x_hbm, raw_a_hbm, bn_a, raw_d_hbm, bn_d, wi_hbm, bn_i, raw_m_hbm, bn_m, raw_o_hbm, bn_o,
+               h_hbm, u_hbm, scale_out, weight_out,
                raw_a, raw_d, wi, raw_m, raw_o, w_sem,
-               perm, wa, wd, wm, wo, xv, xh, hs, us, za, zb, hb, ov, acc, ab, stat,
+               perm, wa, wd, wm, wo, xv, xh, hs, us, za, zb, hb, ub, acc, ab, stat,
                x_sem, out_sem, halo_send, halo_recv, zh, early_send, early_recv, stat_send, stat_recv):
         pairs = xv.shape[0]
         me = lax.axis_index("sp")
         count_a = float(2 * pairs * ROWS_A * LANES * groups)
-        count_b = float(2 * pairs * ROWS_B * 128 * groups)
+        count_b = float(2 * pairs * ROWS_B * HALF * groups)
 
         def sweep(body, *later, before=None, after=None, first=0):
             @pl.loop(first, pairs // UNROLL)
@@ -85,10 +98,10 @@
             return lambda pair: (x_hbm.at[pl.ds(2 * pair, 2 * UNROLL), row], xh.at[slot, pl.ds(2 * pair, 2 * UNROLL)])
 
         def h_part(row, slot):
-            return lambda pair: (hs.at[pl.ds(pair, UNROLL), row, 32:96], hs.at[pl.ds(pair, UNROLL), slot, 32:96])
+            return lambda pair: (hs.at[pl.ds(pair, UNROLL), row, CIN:THREE], hs.at[pl.ds(pair, UNROLL), slot, CIN:THREE])
 
         def u_part(row, slot):
-            return lambda pair: (us.at[pl.ds(pair, UNROLL), row, 64:128], us.at[pl.ds(pair, UNROLL), slot, 64:128])
+            return lambda pair: (us.at[pl.ds(pair, UNROLL), row, MID:HALF], us.at[pl.ds(pair, UNROLL), slot, MID:HALF])
 
         def early_copy(step, side, part, rows, peer):
             return pltpu.make_async_remote_copy(
@@ -153,65 +166,65 @@
             return block.astype(F32).T.astype(BF16)
 
         def prepare_a(layer):
-            for row in range(4):
+            for row in range(FOUR):
                 lines = []
-                for plane in range(4):
+                for plane in range(FOUR):
                     tiles = []
                     for out_row in range(2):
                         for phase in range(2):
                             high, wide = row - out_row, plane - phase
                             inside = 0 <= high < 3 and 0 <= wide < 3
-                            tiles.append(raw_a[layer, high, wide].astype(F32) if inside else jnp.zeros((32, 32), F32))
+                            tiles.append(raw_a[layer, high, wide].astype(F32) if inside else jnp.zeros((CIN, CIN), F32))
                     lines.append(jnp.concatenate(tiles, axis=1))
-                wa[layer, :, 128 * row:128 * row + 128] = turn(jnp.concatenate(lines, axis=0))
+                wa[layer, :, HALF * row:HALF * row + HALF] = turn(jnp.concatenate(lines, axis=0))
 
         def prepare_down():
             for high in range(3):
-                lines = [jnp.zeros((32, 128), BF16)] + [raw_d[high, wide] for wide in range(3)]
-                wd[:, 128 * high:128 * high + 128] = turn(jnp.concatenate(lines, axis=0))
+                lines = [jnp.zeros((CIN, HALF), BF16)] + [raw_d[high, wide] for wide in range(3)]
+                wd[:, HALF * high:HALF * high + HALF] = turn(jnp.concatenate(lines, axis=0))
 
         def prepare_block(block):
             lines = []
-            for row in range(4):
+            for row in range(FOUR):
                 for wide in range(3):
                     tiles = []
                     for out_row in range(2):
                         high = row - out_row
                         inside = 0 <= high < 3
-                        tiles.append(raw_m[block, high, wide].astype(F32) if inside else jnp.zeros((64, 64), F32))
+                        tiles.append(raw_m[block, high, wide].astype(F32) if inside else jnp.zeros((MID, MID), F32))
                     lines.append(jnp.concatenate(tiles, axis=1))
             for part in range(6):
-                wm[block, :, 128 * part:128 * part + 128] = turn(jnp.concatenate(lines[2 * part:2 * part + 2], axis=0))
+                wm[block, :, HALF * part:HALF * part + HALF] = turn(jnp.concatenate(lines[2 * part:2 * part + 2], axis=0))
             wo[block] = turn(raw_o[block])
 
         def shift(value, step):
-            lane = lax.broadcasted_iota(jnp.int32, (value.shape[0], 128), 1)
+            lane = lax.broadcasted_iota(jnp.int32, (value.shape[0], HALF), 1)
             edge = 0 if step == 1 else 127
             halves = []
             for half in range(2):
-                moved = pltpu.roll(value[:, half * 128:(half + 1) * 128], step % 128, 1)
+                moved = pltpu.roll(value[:, half * HALF:(half + 1) * HALF], step % HALF, 1)
                 halves.append(jnp.where(lane == edge, 0.0, moved))
             return jnp.concatenate(halves, axis=1)
 
         def put_planes(pair, row, even, odd, centre=True):
-            hs[pair, row, 0:32] = shift(odd, 1).astype(BF16)
+            hs[pair, row, 0:CIN] = shift(odd, 1).astype(BF16)
             if centre:
-                hs[pair, row, 32:64] = even.astype(BF16)
-                hs[pair, row, 64:96] = odd.astype(BF16)
-            hs[pair, row, 96:128] = shift(even, -1).astype(BF16)
+                hs[pair, row, CIN:MID] = even.astype(BF16)
+                hs[pair, row, MID:THREE] = odd.astype(BF16)
+            hs[pair, row, THREE:HALF] = shift(even, -1).astype(BF16)
 
         def put_mid(pair, row, value, centre=True):
-            us[pair, row, 0:64] = shift(value, 1).astype(BF16)
+            us[pair, row, 0:MID] = shift(value, 1).astype(BF16)
             if centre:
-                us[pair, row, 64:128] = value.astype(BF16)
-            us[pair, row, 128:192] = shift(value, -1).astype(BF16)
+                us[pair, row, MID:HALF] = value.astype(BF16)
+            us[pair, row, HALF:TRIPLE] = shift(value, -1).astype(BF16)
 
         def rebuild_a(pair, row):
-            both = hs[pair, row, 32:96].astype(F32)
-            put_planes(pair, row, both[0:32], both[32:64], centre=False)
+            both = hs[pair, row, CIN:THREE].astype(F32)
+            put_planes(pair, row, both[0:CIN], both[CIN:MID], centre=False)
 
         def rebuild_mid(pair, row):
-            put_mid(pair, row, us[pair, row, 64:128].astype(F32), centre=False)
+            put_mid(pair, row, us[pair, row, MID:HALF].astype(F32), centre=False)
 
         def clear():
             acc[...] = jnp.zeros(acc.shape, F32)
@@ -221,15 +234,15 @@
             for value in values:
                 for half in range(2):
                     for row in range(0, value.shape[0], channels):
-                        piece = value[row:row + channels, half * 128:(half + 1) * 128]
+                        piece = value[row:row + channels, half * HALF:(half + 1) * HALF]
                         total, square = total + piece, square + piece * piece
             return jnp.stack([total, square])
 
         def moments(layer, params, count, during=None, early=None):
             channels = params.shape[1]
             for part in range(2):
-                turned = jnp.concatenate([acc[part, 0:channels]] * (128 // channels), axis=0).T.reshape(16, 8, 128)
-                stat[layer, me, 8 * part:8 * part + 8] = jnp.sum(turned, axis=0)
+                turned = jnp.concatenate([acc[part, 0:channels]] * (HALF // channels), axis=0).T.reshape(PAIR_SUB, SUB, HALF)
+                stat[layer, me, SUB * part:SUB * part + SUB] = jnp.sum(turned, axis=0)
             copies = []
             for hop in range(1, groups):
                 copies.append(pltpu.make_async_remote_copy(
@@ -258,19 +271,19 @@
             def fold(block):
                 return jnp.sum(block, axis=0, keepdims=True) / count
 
-            mean, square = fold(total[0:8]), fold(total[8:16])
+            mean, square = fold(total[0:SUB]), fold(total[SUB:PAIR_SUB])
             var = square - mean * mean
-            wide = jnp.concatenate([params] * (128 // channels), axis=1)
+            wide = jnp.concatenate([params] * (HALF // channels), axis=1)
             scale = wide[0:1] * lax.rsqrt(var + NORM_EPS)
             bias = wide[1:2] - mean * scale
-            ab[0] = jnp.broadcast_to(scale, (128, 128)).T
-            ab[1] = jnp.broadcast_to(bias, (128, 128)).T
+            ab[0] = jnp.broadcast_to(scale, (HALF, HALF)).T
+            ab[1] = jnp.broadcast_to(bias, (HALF, HALF)).T
 
         def affine(value):
             rows = value.shape[0]
             scale, bias = ab[0, 0:rows], ab[1, 0:rows]
             return jnp.concatenate(
-                [value[:, :128] * scale + bias, value[:, 128:] * scale + bias], axis=1)
+                [value[:, :HALF] * scale + bias, value[:, HALF:] * scale + bias], axis=1)
 
         def norm_relu(value):
             return jnp.maximum(affine(value), 0.0)
@@ -284,39 +297,39 @@
 
         lane_in = lax.broadcasted_iota(jnp.int32, (LANES, LANES), 0)
         lane_out = lax.broadcasted_iota(jnp.int32, (LANES, LANES), 1)
-        source = jnp.where(lane_out < 128, 2 * lane_out, 2 * lane_out - (LANES - 1))
+        source = jnp.where(lane_out < HALF, 2 * lane_out, 2 * lane_out - (LANES - 1))
         perm[...] = jnp.where(lane_in == source, 1.0, 0.0).astype(BF16)
 
         def split_rows(first, second, pair, row):
-            put_planes(pair, row, jnp.concatenate([first[:, :128], second[:, :128]], axis=1),
-                       jnp.concatenate([first[:, 128:], second[:, 128:]], axis=1))
+            put_planes(pair, row, jnp.concatenate([first[:, :HALF], second[:, :HALF]], axis=1),
+                       jnp.concatenate([first[:, HALF:], second[:, HALF:]], axis=1))
 
         def conv_a(layer, pair, row, rows):
-            window = hs[pair, row:row + rows + 2].reshape((rows + 2) * 128, LANES)
-            value = mm(wa[layer, 0:64 * rows, 0:128 * (rows + 2)], window)
-            za[pl.ds(pair * ROWS_A + row, rows)] = value.reshape(rows, 64, LANES)
+            window = hs[pair, row:row + rows + 2].reshape((rows + 2) * HALF, LANES)
+            value = mm(wa[layer, 0:MID * rows, 0:HALF * (rows + 2)], window)
+            za[pl.ds(pair * ROWS_A + row, rows)] = value.reshape(rows, MID, LANES)
             return value
 
         def norm_a(pair, row):
             value = norm_relu(za[pair * ROWS_A + row])
-            put_planes(pair, row + 1, value[0:32], value[32:64])
+            put_planes(pair, row + 1, value[0:CIN], value[CIN:MID])
 
         def planes(pair):
             x_copy(pair).wait()
-            both = mm(xv[pair].reshape(2 * ROWS_A * 32, LANES), perm[...]).reshape(2, ROWS_A, 32, LANES)
+            both = mm(xv[pair].reshape(2 * ROWS_A * CIN, LANES), perm[...]).reshape(2, ROWS_A, CIN, LANES)
             for row in range(ROWS_A):
                 split_rows(both[0, row], both[1, row], pair, row + 1)
 
         def inner_a(layer):
-            return lambda pair: tally(32, *[conv_a(layer, pair, row, 2) for row in range(1, ROWS_A - 1, 2)])
+            return lambda pair: tally(CIN, *[conv_a(layer, pair, row, 2) for row in range(1, ROWS_A - 1, 2)])
 
         def outer_a(layer):
-            return lambda pair: tally(32, conv_a(layer, pair, 0, 1), conv_a(layer, pair, ROWS_A - 1, 1))
+            return lambda pair: tally(CIN, conv_a(layer, pair, 0, 1), conv_a(layer, pair, ROWS_A - 1, 1))
 
         sweep(planes, inner_a(0))
 
         def halo_planes(pair):
-            both = mm(xh[:, pl.ds(2 * pair, 2)].reshape(4 * 32, LANES), perm[...]).reshape(2, 2, 32, LANES)
+            both = mm(xh[:, pl.ds(2 * pair, 2)].reshape(FOUR * CIN, LANES), perm[...]).reshape(2, 2, CIN, LANES)
             split_rows(both[0, 0], both[0, 1], pair, 0)
             split_rows(both[1, 0], both[1, 1], pair, ROWS_A + 1)
 
@@ -334,7 +347,7 @@
             norm_a(pair, ROWS_A - 1)
 
         def put_edge(pair, slot, value):
-            put_planes(pair, slot, value[0:32], value[32:64])
+            put_planes(pair, slot, value[0:CIN], value[CIN:MID])
 
         sweep(norm_edges, after=lambda chunk: exchange(1, h_refs, chunk), first=1)
         first_chunk(norm_edges)
@@ -356,7 +369,7 @@
         moments(1, bn_a[1], count_a, prepare_down, lambda: early(2, ROWS_A, (1,)))
 
         def conv_down(pair, row):
-            window = hs[pair, 2 * row + 1:2 * row + 4].reshape(384, LANES)
+            window = hs[pair, 2 * row + 1:2 * row + FOUR].reshape(DOWN_K, LANES)
             value = mm(wd[...], window)
             zb[pair * ROWS_B + row] = value
             return value
@@ -368,10 +381,10 @@
             for row in range(1, ROWS_A):
                 norm_a(pair, row)
 
-        sweep(norm_below, lambda pair: tally(128, *[conv_down(pair, row) for row in range(ROWS_B - 1)]))
+        sweep(norm_below, lambda pair: tally(HALF, *[conv_down(pair, row) for row in range(ROWS_B - 1)]))
 
         def down_edge(pair):
-            return tally(128, conv_down(pair, ROWS_B - 1))
+            return tally(HALF, conv_down(pair, ROWS_B - 1))
 
         settle_early(2, ROWS_A, put_edge, (1,))
         first_chunk(down_edge)
@@ -386,16 +399,16 @@
             return value
 
         def conv_mid(block, pair, row, rows):
-            window = us[pair, row:row + rows + 2].reshape((rows + 2) * 192, LANES)
-            value = mm(wm[block, 0:64 * rows, 0:192 * (rows + 2)], window)
-            za[pl.ds(pair * ROWS_B + row, rows)] = value.reshape(rows, 64, LANES)
+            window = us[pair, row:row + rows + 2].reshape((rows + 2) * TRIPLE, LANES)
+            value = mm(wm[block, 0:MID * rows, 0:TRIPLE * (rows + 2)], window)
+            za[pl.ds(pair * ROWS_B + row, rows)] = value.reshape(rows, MID, LANES)
             return value
 
         def norm_mid(pair, row):
             put_mid(pair, row + 1, norm_relu(za[pair * ROWS_B + row]))
 
         def all_in(block):
-            return lambda pair: tally(64, *[conv_in(block, pair * ROWS_B + row) for row in range(ROWS_B)])
+            return lambda pair: tally(MID, *[conv_in(block, pair * ROWS_B + row) for row in range(ROWS_B)])
 
         def first_hidden(pair):
             for row in range(ROWS_B):
@@ -415,7 +428,7 @@
                 norm_mid(pair, ROWS_B - 1)
 
             def mid_conv(pair):
-                return tally(64, conv_mid(block, pair, 0, 1), conv_mid(block, pair, ROWS_B - 1, 1))
+                return tally(MID, conv_mid(block, pair, 0, 1), conv_mid(block, pair, ROWS_B - 1, 1))
 
             sweep(mid_edges, after=lambda chunk: exchange(step, u_refs, chunk), first=1)
             first_chunk(mid_edges)
@@ -428,49 +441,87 @@
                 rebuild_mid(pair, 0)
                 rebuild_mid(pair, ROWS_B + 1)
 
-            sweep(mid_inner, lambda pair: tally(64, conv_mid(block, pair, 1, 2)))
+            sweep(mid_inner, lambda pair: tally(MID, conv_mid(block, pair, 1, 2)))
             settle_early(step, ROWS_B, put_mid)
             first_chunk(mid_conv)
             sweep(mid_outer, mid_conv, before=lambda chunk: settle(step, u_refs, chunk), first=1)
 
             moments(layer + 1, bn_m[block], count_b)
 
-            @sweep
-            def _(pair):
+            last = block == blocks - 1
+            if last:
+                h_copy = pltpu.make_async_copy(hb, h_hbm, out_sem.at[pairs // UNROLL])
+                h_copy.start()
+                weight_out[...] = wo[block]
+
+            def u_copy(chunk):
+                span = pl.ds(chunk * UNROLL * ROWS_B, UNROLL * ROWS_B)
+                return pltpu.make_async_copy(ub.at[span], u_hbm.at[span], out_sem.at[chunk])
+
+            def all_out(pair):
                 values = []
                 for row in range(ROWS_B):
                     index = pair * ROWS_B + row
-                    values.append(mm(wo[block], norm_relu(za[index]).astype(BF16)))
-                    zb[index] = values[-1]
-                return tally(128, *values)
-
+                    hidden = norm_relu(za[index]).astype(BF16)
+                    values.append(mm(wo[block], hidden))
+                    if last:
+                        ub[index] = hidden
+                    else:
+                        zb[index] = values[-1]
+                return tally(HALF, *values)
+
+            sweep(all_out, after=(lambda chunk: u_copy(chunk).start()) if last else None)
             moments(layer + 2, bn_o[block], count_b)
 
-            def finish(index):
-                return jnp.maximum(affine(zb[index]) + hb[index].astype(F32), 0.0)
-
-            if block < blocks - 1:
+            if not last:
                 def next_hidden(pair):
                     for row in range(ROWS_B):
                         index = pair * ROWS_B + row
-                        hb[index] = finish(index).astype(BF16)
+                        hb[index] = jnp.maximum(affine(zb[index]) + hb[index].astype(F32), 0.0).astype(BF16)
 
                 sweep(next_hidden, all_in(block + 1))
             else:
-                def out_copy(pair):
-                    return pltpu.make_async_copy(ov.at[pair], out_hbm.at[pl.ds(2 * pair, 2)], out_sem.at[pair])
-
-                @sweep
-                def _(pair):
-                    for row in range(ROWS_B):
-                        value = finish(pair * ROWS_B + row)
-                        for image in range(2):
-                            ov[pair, image, row] = value[:, image * 128:(image + 1) * 128].T.astype(BF16)
-                    out_copy(pair).start()
-
-                @sweep
-                def _(pair):
-                    out_copy(pair).wait()
+                scale_out[...] = ab[...]
+                h_copy.wait()
+
+                @pl.loop(0, pairs // UNROLL)
+                def _(chunk):
+                    u_copy(chunk).wait()
+
+    def last_kernel(h_hbm, u_hbm, scale_ref, weight_ref, out_hbm, hv, uv, ov, h_sem, u_sem, out_sem):
+        chunks = h_sem.shape[0]
+        span = hv.shape[0] // chunks
+
+        def loads(chunk):
+            part = pl.ds(chunk * span, span)
+            return (pltpu.make_async_copy(h_hbm.at[part], hv.at[part], h_sem.at[chunk]),
+                    pltpu.make_async_copy(u_hbm.at[part], uv.at[part], u_sem.at[chunk]))
+
+        def store(chunk):
+            part = pl.ds(chunk * 2 * (span // ROWS_B), 2 * (span // ROWS_B))
+            return pltpu.make_async_copy(ov.at[part], out_hbm.at[part], out_sem.at[chunk])
+
+        for chunk in range(chunks):
+            for load in loads(chunk):
+                load.start()
+
+        @pl.loop(0, chunks)
+        def _(chunk):
+            for load in loads(chunk):
+                load.wait()
+            scale, bias, weight = scale_ref[0], scale_ref[1], weight_ref[...]
+            for tile in range(span):
+                value = jnp.dot(weight, uv[chunk * span + tile], preferred_element_type=F32)
+                hidden = hv[chunk * span + tile].astype(F32)
+                for image in range(2):
+                    half = slice(image * HALF, (image + 1) * HALF)
+                    done = jnp.maximum(value[:, half] * scale + bias + hidden[:, half], 0.0)
+                    ov[chunk * 2 * (span // ROWS_B) + 2 * (tile // ROWS_B) + image, tile % ROWS_B] = done.T.astype(BF16)
+            store(chunk).start()
+
+        @pl.loop(0, chunks)
+        def _(chunk):
+            store(chunk).wait()
 
     def forward(images, w_a, bn_a, w_down, bn_down, w_in, bn_in, w_mid, bn_mid, w_out, bn_out):
         images_count = images.shape[0]
@@ -481,38 +532,52 @@
         vmem = pl.BlockSpec(memory_space=pltpu.VMEM)
         hbm = pl.BlockSpec(memory_space=pl.ANY)
         dma = pltpu.SemaphoreType.DMA
-        return pl.pallas_call(
+        tiles = pairs * ROWS_B
+        hidden, branch, scale, weight = pl.pallas_call(
             kernel,
-            out_shape=jax.ShapeDtypeStruct((images_count, ROWS_B, 128, 128), BF16),
+            out_shape=(
+                jax.ShapeDtypeStruct((tiles, HALF, LANES), BF16), jax.ShapeDtypeStruct((tiles, MID, LANES), BF16),
+                jax.ShapeDtypeStruct((2, HALF, HALF), F32), jax.ShapeDtypeStruct((HALF, MID), BF16)),
             in_specs=[hbm] + [hbm, vmem] * 5,
-            out_specs=hbm,
+            out_specs=(hbm, hbm, vmem, vmem),
             scratch_shapes=[
-                pltpu.VMEM(w_a.shape, BF16), pltpu.VMEM(w_down.shape, BF16), pltpu.VMEM((w_in.shape[0], 64, 128), BF16),
+                pltpu.VMEM(w_a.shape, BF16), pltpu.VMEM(w_down.shape, BF16), pltpu.VMEM((w_in.shape[0], MID, HALF), BF16),
                 pltpu.VMEM(w_mid.shape, BF16), pltpu.VMEM(w_out.shape, BF16), dma((5,)),
                 pltpu.VMEM((LANES, LANES), BF16),
-                pltpu.VMEM((w_a.shape[0], 128, 512), BF16),
-                pltpu.VMEM((128, 384), BF16),
-                pltpu.VMEM((w_in.shape[0], 128, 768), BF16),
-                pltpu.VMEM((w_in.shape[0], 128, 64), BF16),
-                pltpu.VMEM((pairs, 2, ROWS_A, 32, LANES), BF16),
-                pltpu.VMEM((2, images_count, 32, LANES), BF16),
-                pltpu.VMEM((pairs, ROWS_A + 2, 128, LANES), BF16),
-                pltpu.VMEM((pairs, ROWS_B + 2, 192, LANES), BF16),
-                pltpu.VMEM((pairs * ROWS_A, 64, LANES), F32),
-                pltpu.VMEM((pairs * ROWS_B, 128, LANES), F32),
-                pltpu.VMEM((pairs * ROWS_B, 128, LANES), BF16),
-                pltpu.VMEM((pairs, 2, ROWS_B, 128, 128), BF16),
-                pltpu.VMEM((2, 128, 128), F32),
-                pltpu.VMEM((2, 128, 128), F32),
-                pltpu.VMEM((layers, groups, 16, 128), F32),
-                dma((pairs,)), dma((pairs,)), dma((steps, 2, pairs // UNROLL)), dma((steps, 2, pairs // UNROLL)),
-                pltpu.VMEM((steps, 2, UNROLL, 64, LANES), F32), dma((steps, 2, UNROLL)), dma((steps, 2, UNROLL)),
+                pltpu.VMEM((w_a.shape[0], HALF, BAND_A), BF16),
+                pltpu.VMEM((HALF, DOWN_K), BF16),
+                pltpu.VMEM((w_in.shape[0], HALF, BAND_B), BF16),
+                pltpu.VMEM((w_in.shape[0], HALF, MID), BF16),
+                pltpu.VMEM((pairs, 2, ROWS_A, CIN, LANES), BF16),
+                pltpu.VMEM((2, images_count, CIN, LANES), BF16),
+                pltpu.VMEM((pairs, ROWS_A + 2, HALF, LANES), BF16),
+                pltpu.VMEM((pairs, ROWS_B + 2, TRIPLE, LANES), BF16),
+                pltpu.VMEM((pairs * ROWS_A, MID, LANES), F32),
+                pltpu.VMEM((pairs * ROWS_B, HALF, LANES), F32),
+                pltpu.VMEM((pairs * ROWS_B, HALF, LANES), BF16),
+                pltpu.VMEM((pairs * ROWS_B, MID, LANES), BF16),
+                pltpu.VMEM((2, HALF, HALF), F32),
+                pltpu.VMEM((2, HALF, HALF), F32),
+                pltpu.VMEM((layers, groups, PAIR_SUB, HALF), F32),
+                dma((pairs,)), dma((pairs // UNROLL + 1,)), dma((steps, 2, pairs // UNROLL)), dma((steps, 2, pairs // UNROLL)),
+                pltpu.VMEM((steps, 2, UNROLL, MID, LANES), F32), dma((steps, 2, UNROLL)), dma((steps, 2, UNROLL)),
                 dma((layers, groups)), dma((layers, groups)),
             ],
             compiler_params=pltpu.CompilerParams(
                 collective_id=0, has_side_effects=True, vmem_limit_bytes=67043328),
             name="conv_stack",
         )(x, w_a, bn_a, w_down, bn_down, jnp.transpose(w_in, (0, 2, 1)), bn_in, w_mid, bn_mid, w_out, bn_out)
+        return pl.pallas_call(
+            last_kernel,
+            out_shape=jax.ShapeDtypeStruct((images_count, ROWS_B, HALF, HALF), BF16),
+            in_specs=[hbm, hbm, vmem, vmem],
+            out_specs=hbm,
+            scratch_shapes=[
+                pltpu.VMEM((tiles, HALF, LANES), BF16), pltpu.VMEM((tiles, MID, LANES), BF16),
+                pltpu.VMEM((images_count, ROWS_B, HALF, HALF), BF16),
+                dma((LAST_STEPS,)), dma((LAST_STEPS,)), dma((LAST_STEPS,))],
+            name="last_layer",
+        )(hidden, branch, scale, weight)
 
     act_spec = P("dp", "sp", None, None)
     return jax.shard_map(forward, mesh=mesh, in_specs=(act_spec,) + (P(),) * 10, out_specs=act_spec, check_vma=False)

time: 109 us -> 107 us (0.982)
  local copies, waits for them, and re-layouts: 4.79 us -> 0 us
  Pallas kernels: 104 us -> 107 us
    unnamed x1 -> x0, local copies, waits for them, and re-layouts: 4.79 us -> none
    pallas_call x1 -> x2, Pallas kernels: 104 us -> 107 us  [the longest x1 101 us: forward(): pl.pallas_call(kernel, out_shape=(jax.ShapeDtypeStruct((tiles, HALF, LANE...]
where the time goes in v6:
time: 107 us
  Pallas kernels  107 us (100%)
    pallas_call x1, Pallas kernels, forward(): pl.pallas_call(kernel, out_shape=(jax.ShapeDtypeStruct((tiles, HALF, LANE...  101 us
    pallas_call x1, Pallas kernels, forward(): pl.pallas_call(last_kernel, out_shape=jax.ShapeDtypeStruct((images_count,...  6 us

profile of v6, /device:TPU:0, one launch (start us, length us, event | category | flops | bytes accessed | tf_op | source)
XLA Modules:
  0.0 107.3 jit_solution(2518067746458028098)
XLA Ops:
  0.0 101.2 %conv_stack.1 = (bf16[64,128,256]{2,1,0:T(8,128)(2,1)}, bf16[64,64,256]{2,1,0:T(8,128)(2,1)}, f32[2,128,128]{2,1,0:T(8,128)}, bf16[128,64]{1,0:T(8,128)(2,1)}) custom-call(bf16[32,8,32,256]{3,2,1,0:T(8,128)(2,1)} %bitcast.2, bf16[2,3,3,32,32]{4,3,2,1,0:T(8,128)(2,1)} %raw_a_hbm.1, f32[2,2,32]{2,1,0:T(2,128)} %bn_a.1, bf16[3,3,32,128]{3,2,1,0:T(8,128)(2,1)} %raw_d_hbm.1, ...), custom_call_target="tpu_custom_call" | custom-call | tf_op jit(solution)/shard_map/conv_stack/pallas_call | solution.py:536
  101.2 6.0 %last_layer.1 = bf16[32,4,128,128]{3,2,1,0:T(8,128)(2,1)} custom-call(bf16[64,128,256]{2,1,0:T(8,128)(2,1)} %get-tuple-element.9.h_hbm, bf16[64,64,256]{2,1,0:T(8,128)(2,1)} %get-tuple-element.10.u_hbm, f32[2,128,128]{2,1,0:T(8,128)} %get-tuple-element.11.scale_ref, bf16[128,64]{1,0:T(8,128)(2,1)} %get-tuple-element.12.weight_ref), custom_call_target="tpu_custom_call" | custom-call | tf_op jit(solution)/shard_map/last_layer/pallas_call | solution.py:570

commit v7 on v6

--- a/solution.py
+++ b/solution.py
@@ -183,18 +183,20 @@
                 lines = [jnp.zeros((CIN, HALF), BF16)] + [raw_d[high, wide] for wide in range(3)]
                 wd[:, HALF * high:HALF * high + HALF] = turn(jnp.concatenate(lines, axis=0))
 
-        def prepare_block(block):
-            lines = []
-            for row in range(FOUR):
-                for wide in range(3):
+        def prepare_mid(block, parts):
+            for part in parts:
+                lines = []
+                for line in (2 * part, 2 * part + 1):
+                    row, wide = divmod(line, 3)
                     tiles = []
                     for out_row in range(2):
                         high = row - out_row
                         inside = 0 <= high < 3
                         tiles.append(raw_m[block, high, wide].astype(F32) if inside else jnp.zeros((MID, MID), F32))
                     lines.append(jnp.concatenate(tiles, axis=1))
-            for part in range(6):
-                wm[block, :, HALF * part:HALF * part + HALF] = turn(jnp.concatenate(lines[2 * part:2 * part + 2], axis=0))
+                wm[block, :, HALF * part:HALF * part + HALF] = turn(jnp.concatenate(lines, axis=0))
+
+        def prepare_out(block):
             wo[block] = turn(raw_o[block])
 
         def shift(value, step):
@@ -316,9 +318,11 @@
 
         def planes(pair):
             x_copy(pair).wait()
-            both = mm(xv[pair].reshape(2 * ROWS_A * CIN, LANES), perm[...]).reshape(2, ROWS_A, CIN, LANES)
-            for row in range(ROWS_A):
-                split_rows(both[0, row], both[1, row], pair, row + 1)
+            for start in range(0, ROWS_A, FOUR):
+                both = mm(xv[pair, :, start:start + FOUR].reshape(2 * FOUR * CIN, LANES), perm[...])
+                both = both.reshape(2, FOUR, CIN, LANES)
+                for row in range(FOUR):
+                    split_rows(both[0, row], both[1, row], pair, start + row + 1)
 
         def inner_a(layer):
             return lambda pair: tally(CIN, *[conv_a(layer, pair, row, 2) for row in range(1, ROWS_A - 1, 2)])
@@ -339,6 +343,11 @@
             for load in loads[1:]:
                 load.wait()
             prepare_a(1)
+            prepare_mid(0, (0, 1))
+
+        def down_weights():
+            prepare_down()
+            prepare_mid(0, (2, 3))
 
         moments(0, bn_a[0], count_a, second_weights, lambda: early(1, ROWS_A))
 
@@ -366,7 +375,7 @@
         first_chunk(outer_a(1))
         sweep(rebuild_both, outer_a(1), before=lambda chunk: settle(1, h_refs, chunk), first=1)
 
-        moments(1, bn_a[1], count_a, prepare_down, lambda: early(2, ROWS_A, (1,)))
+        moments(1, bn_a[1], count_a, down_weights, lambda: early(2, ROWS_A, (1,)))
 
         def conv_down(pair, row):
             window = hs[pair, 2 * row + 1:2 * row + FOUR].reshape(DOWN_K, LANES)
@@ -391,7 +400,7 @@
         sweep(lambda pair: rebuild_a(pair, ROWS_A + 1), down_edge,
               before=lambda chunk: settle(2, h_refs, chunk, (1,)), first=1)
 
-        moments(2, bn_d[...], count_b, lambda: prepare_block(0))
+        moments(2, bn_d[...], count_b, lambda: prepare_mid(0, (FOUR, 5)))
 
         def conv_in(block, index):
             value = mm(wi[block], hb[index])
@@ -420,7 +429,7 @@
         blocks = wi.shape[0]
         for block in range(blocks):
             layer, step = 3 + 3 * block, 3 + block
-            moments(layer, bn_i[block], count_b, (lambda: prepare_block(block + 1)) if block < blocks - 1 else None,
+            moments(layer, bn_i[block], count_b, lambda: prepare_out(block),
                     lambda: early(step, ROWS_B))
 
             def mid_edges(pair):
@@ -446,9 +455,9 @@
             first_chunk(mid_conv)
             sweep(mid_outer, mid_conv, before=lambda chunk: settle(step, u_refs, chunk), first=1)
 
-            moments(layer + 1, bn_m[block], count_b)
-
             last = block == blocks - 1
+            moments(layer + 1, bn_m[block], count_b, None if last else lambda: prepare_mid(block + 1, (0, 1, 2)))
+
             if last:
                 h_copy = pltpu.make_async_copy(hb, h_hbm, out_sem.at[pairs // UNROLL])
                 h_copy.start()
@@ -471,7 +480,7 @@
                 return tally(HALF, *values)
 
             sweep(all_out, after=(lambda chunk: u_copy(chunk).start()) if last else None)
-            moments(layer + 2, bn_o[block], count_b)
+            moments(layer + 2, bn_o[block], count_b, None if last else lambda: prepare_mid(block + 1, (3, FOUR, 5)))
 
             if not last:
                 def next_hidden(pair):

time: 107 us -> 106 us (level)
  no operation moved by 1% of the time
where the time goes in v7:
time: 106 us
  Pallas kernels  106 us (100%)
    pallas_call x1, Pallas kernels, forward(): pl.pallas_call(kernel, out_shape=(jax.ShapeDtypeStruct((tiles, HALF, LANE...  100 us
    pallas_call x1, Pallas kernels, forward(): pl.pallas_call(last_kernel, out_shape=jax.ShapeDtypeStruct((images_count,...  6 us

profile of v7, /device:TPU:0, one launch (start us, length us, event | category | flops | bytes accessed | tf_op | source)
XLA Modules:
  0.0 106.3 jit_solution(9399358198107588185)
XLA Ops:
  0.0 100.2 %conv_stack.1 = (bf16[64,128,256]{2,1,0:T(8,128)(2,1)}, bf16[64,64,256]{2,1,0:T(8,128)(2,1)}, f32[2,128,128]{2,1,0:T(8,128)}, bf16[128,64]{1,0:T(8,128)(2,1)}) custom-call(bf16[32,8,32,256]{3,2,1,0:T(8,128)(2,1)} %bitcast.2, bf16[2,3,3,32,32]{4,3,2,1,0:T(8,128)(2,1)} %raw_a_hbm.1, f32[2,2,32]{2,1,0:T(2,128)} %bn_a.1, bf16[3,3,32,128]{3,2,1,0:T(8,128)(2,1)} %raw_d_hbm.1, ...), custom_call_target="tpu_custom_call" | custom-call | tf_op jit(solution)/shard_map/conv_stack/pallas_call | solution.py:545
  100.2 6.0 %last_layer.1 = bf16[32,4,128,128]{3,2,1,0:T(8,128)(2,1)} custom-call(bf16[64,128,256]{2,1,0:T(8,128)(2,1)} %get-tuple-element.9.h_hbm, bf16[64,64,256]{2,1,0:T(8,128)(2,1)} %get-tuple-element.10.u_hbm, f32[2,128,128]{2,1,0:T(8,128)} %get-tuple-element.11.scale_ref, bf16[128,64]{1,0:T(8,128)(2,1)} %get-tuple-element.12.weight_ref), custom_call_target="tpu_custom_call" | custom-call | tf_op jit(solution)/shard_map/last_layer/pallas_call | solution.py:579
